TPU v7x, 64 devices: a 2x2x8 block of a 4x4x8 slice. The times are simulated.
64 devices in a mesh: rep: 8 (over x, y, core), dp: 8 (over z).
Axes of the slice: x: 2, y: 2, z: 8, core: 2. Of those that a mesh axis runs over, the one named last changes fastest.
The devices are a block of a 4x4x8 slice.
Arguments:
- g_w_gate: bfloat16 [64, 2, 512, 1280], P(('rep', 'dp')), parts along dimension 0
- g_w_up: bfloat16 [64, 2, 512, 1280], P(('rep', 'dp')), parts along dimension 0
- g_w_down: bfloat16 [64, 2, 1280, 512], P(('rep', 'dp')), parts along dimension 0
- w_gate: bfloat16 [2, 512, 1280], replicated
- w_up: bfloat16 [2, 512, 1280], replicated
- w_down: bfloat16 [2, 1280, 512], replicated
- m_w_gate: float32 [2, 512, 1280], P(None, 'dp')
- m_w_up: float32 [2, 512, 1280], P(None, 'dp')
- m_w_down: float32 [2, 1280, 512], P(None, 'dp')
- v_w_gate: float32 [2, 512, 1280], P(None, 'dp')
- v_w_up: float32 [2, 512, 1280], P(None, 'dp')
- v_w_down: float32 [2, 1280, 512], P(None, 'dp')
Outputs:
- output 1: bfloat16 [16, 512, 1280], P('rep'), parts along dimension 0
- output 2: bfloat16 [16, 512, 1280], P('rep'), parts along dimension 0
- output 3: bfloat16 [16, 1280, 512], P('rep'), parts along dimension 0
- output 4: float32 [16, 512, 1280], P('rep', 'dp'), parts along dimension 0
- output 5: float32 [16, 512, 1280], P('rep', 'dp'), parts along dimension 0
- output 6: float32 [16, 1280, 512], P('rep', 'dp'), parts along dimension 0
- output 7: float32 [16, 512, 1280], P('rep', 'dp'), parts along dimension 0
- output 8: float32 [16, 512, 1280], P('rep', 'dp'), parts along dimension 0
- output 9: float32 [16, 1280, 512], P('rep', 'dp'), parts along dimension 0
There are 8 independent parts. A program takes and returns all parts, laid end to end along the dimension named above; an argument that names none is the same for every part.
All inputs are finite; a program needn't handle non-finite values.
Results may differ from a plain program's by a relative error of at most 0.022.
Values are sent between devices in bfloat16 or wider.
A program may use at most 768 MiB of HBM per device.

v0:
```python
import jax
import jax.numpy as jnp
from jax import lax
from jax.sharding import PartitionSpec as P


def adamw(w, m, v, g):
    m = 0.9 * m + 0.1 * g
    v = 0.95 * v + 0.05 * g * g
    step = m * lax.rsqrt(v + 1e-8) + 0.1 * w
    return (w - 0.02 * step).astype(jnp.bfloat16), m, v


def solution(mesh):
    def step(*arrays):
        terms, weights, m, v = (arrays[i : i + 3] for i in (0, 3, 6, 9))
        gradients = [lax.psum_scatter(t[0], "dp", scatter_dimension=1, tiled=True).astype(jnp.float32) for t in terms]
        me = lax.axis_index("dp")
        own = [lax.dynamic_slice_in_dim(w, me * one.shape[1], one.shape[1], 1).astype(jnp.float32) for w, one in zip(weights, m, strict=True)]
        new = [adamw(w, m, v, g) for w, m, v, g in zip(own, m, v, gradients, strict=True)]
        whole = [lax.all_gather(one[0], "dp", axis=1, tiled=True) for one in new]
        return (*whole, *(one[1] for one in new), *(one[2] for one in new))

    all_of, cut = P(None, None, None), P(None, "dp", None)
    return jax.shard_map(
        step,
        mesh=mesh,
        in_specs=(P(("rep", "dp"), None, None, None),) * 3 + (all_of,) * 3 + (cut,) * 6,
        out_specs=(P("rep", None, None),) * 3 + (P("rep", "dp", None),) * 6,
        check_vma=False,
    )
```

profile of v0, /device:TPU:22, one launch (start us, length us, event | category | flops | bytes accessed | tf_op | source)
XLA Modules:
  0.0 274.9 jit_solution(1604687688885091762)
XLA Ops:
  7.2 0.1 reduce-scatter.8.cloned.1.call-start
  7.3 0.7 reduce-scatter.8.cloned.1.call-update
  8.0 0.1 reduce-scatter.6.cloned.1.call-start
  8.1 0.0 copy-start.2
  8.1 0.0 copy-start.3
  8.1 0.7 reduce-scatter.6.cloned.1.call-update
  8.8 0.1 reduce-scatter.4.cloned.1.call-start
  8.9 0.7 reduce-scatter.4.cloned.1.call-update
  9.6 0.0 copy-start.4
  9.6 0.0 copy-start.5
  9.6 0.1 all-gather.8.cloned.1.call-start
  9.7 45.5 %reduce-scatter.8.cloned.1.call-done = bf16[2,160,512]{2,1,0:T(8,128)(2,1)} async-done(((bf16[2,1280,512]{2,1,0:T(8,128)(2,1)}), bf16[2,160,512]{2,1,0:T(8,128)(2,1)}) %reduce-scatter.8.cloned.1.call-update) | async-done | bytes 327696 | tf_op jit(solution)/shard_map/reduce_scatter | solution.py:17
  55.2 0.0 copy-done.2
  55.2 2.4 fusion.10
  57.7 0.1 all-gather.8.cloned.1.call-update
  57.7 0.1 all-gather.6.cloned.1.call-start
  57.8 40.1 %reduce-scatter.6.cloned.1.call-done = bf16[2,64,1280]{2,1,0:T(8,128)(2,1)} async-done(((bf16[2,512,1280]{2,1,0:T(8,128)(2,1)}), bf16[2,64,1280]{2,1,0:T(8,128)(2,1)}) %reduce-scatter.6.cloned.1.call-update) | async-done | bytes 327696 | tf_op jit(solution)/shard_map/reduce_scatter | solution.py:17
  97.9 2.4 fusion.6
  100.2 0.1 all-gather.6.cloned.1.call-update
  100.3 0.1 all-gather.4.cloned.1.call-start
  100.4 40.1 %reduce-scatter.4.cloned.1.call-done = bf16[2,64,1280]{2,1,0:T(8,128)(2,1)} async-done(((bf16[2,512,1280]{2,1,0:T(8,128)(2,1)}), bf16[2,64,1280]{2,1,0:T(8,128)(2,1)}) %reduce-scatter.4.cloned.1.call-update) | async-done | bytes 327696 | tf_op jit(solution)/shard_map/reduce_scatter | solution.py:17
  140.5 0.0 copy-done.7
  140.5 2.4 fusion.2
  142.9 0.1 all-gather.4.cloned.1.call-update
  142.9 38.0 %all-gather.8.cloned.1.call-done = bf16[2,1280,512]{2,1,0:T(8,128)(2,1)} async-done(((bf16[2,160,512]{2,1,0:T(8,128)(2,1)}), bf16[2,1280,512]{2,1,0:T(8,128)(2,1)}) %all-gather.8.cloned.1.call-update) | async-done | bytes 2621456 | tf_op jit(solution)/shard_map/all_gather | solution.py:21
  180.9 39.7 %all-gather.6.cloned.1.call-done = bf16[2,512,1280]{2,1,0:T(8,128)(2,1)} async-done(((bf16[2,64,1280]{2,1,0:T(8,128)(2,1)}), bf16[2,512,1280]{2,1,0:T(8,128)(2,1)}) %all-gather.6.cloned.1.call-update) | async-done | bytes 2621456 | tf_op jit(solution)/shard_map/all_gather | solution.py:21
  220.6 39.7 %all-gather.4.cloned.1.call-done = bf16[2,512,1280]{2,1,0:T(8,128)(2,1)} async-done(((bf16[2,64,1280]{2,1,0:T(8,128)(2,1)}), bf16[2,512,1280]{2,1,0:T(8,128)(2,1)}) %all-gather.4.cloned.1.call-update) | async-done | bytes 2621456 | tf_op jit(solution)/shard_map/all_gather | solution.py:21
  260.3 3.5 %copy.24 = bf16[2,512,1280]{2,1,0:T(8,128)(2,1)} copy(bf16[2,512,1280]{2,1,0:T(8,128)(2,1)} %all-gather.4.cloned.1.call-done) | data formatting | bytes 5242880
  263.9 0.0 copy-done.1
  263.9 1.5 copy.25
  265.4 1.2 copy-done
  266.5 1.5 copy.26
  (8 shorter events, 0.0 us)
Async XLA Ops:
  7.2 48.0 %reduce-scatter.8.cloned.1.call-start = ((), (), s32[]{:S(2)}) async-start(), calls=%async_computation.7 | async-start | bytes 2949120 | tf_op jit(solution)/shard_map/reduce_scatter | solution.py:17
  8.0 89.9 %reduce-scatter.6.cloned.1.call-start = ((), (), s32[]{:S(2)}) async-start(), calls=%async_computation.5 | async-start | bytes 2949120 | tf_op jit(solution)/shard_map/reduce_scatter | solution.py:17
  8.1 47.2 %copy-start.2 = (f32[2,160,512]{2,1,0:T(8,128)S(1)}, f32[2,160,512]{2,1,0:T(8,128)}, u32[]{:S(2)}) copy-start(f32[2,160,512]{2,1,0:T(8,128)} %param.23) | copy-start | bytes 1966084
  8.1 47.2 %copy-start.3 = (f32[2,160,512]{2,1,0:T(8,128)S(1)}, f32[2,160,512]{2,1,0:T(8,128)}, u32[]{:S(2)}) copy-start(f32[2,160,512]{2,1,0:T(8,128)} %param.20) | copy-start | bytes 1966084
  8.8 131.7 %reduce-scatter.4.cloned.1.call-start = ((), (), s32[]{:S(2)}) async-start(), calls=%async_computation.3 | async-start | bytes 2949120 | tf_op jit(solution)/shard_map/reduce_scatter | solution.py:17
  9.6 88.3 %copy-start.4 = (f32[2,64,1280]{2,1,0:T(8,128)S(1)}, f32[2,64,1280]{2,1,0:T(8,128)}, u32[]{:S(2)}) copy-start(f32[2,64,1280]{2,1,0:T(8,128)} %param.22) | copy-start | bytes 1966084
  9.6 88.3 %copy-start.5 = (f32[2,64,1280]{2,1,0:T(8,128)S(1)}, f32[2,64,1280]{2,1,0:T(8,128)}, u32[]{:S(2)}) copy-start(f32[2,64,1280]{2,1,0:T(8,128)} %param.19) | copy-start | bytes 1966084
  9.6 171.3 %all-gather.8.cloned.1.call-start = ((), (), s32[]{:S(2)}) async-start(), calls=%async_computation.8 | async-start | bytes 2949120 | tf_op jit(solution)/shard_map/all_gather | solution.py:21
  57.7 82.8 %copy-start.6 = (f32[2,64,1280]{2,1,0:T(8,128)S(1)}, f32[2,64,1280]{2,1,0:T(8,128)}, u32[]{:S(2)}) copy-start(f32[2,64,1280]{2,1,0:T(8,128)} %param.21) | copy-start | bytes 1966084
  57.7 82.8 %copy-start.7 = (f32[2,64,1280]{2,1,0:T(8,128)S(1)}, f32[2,64,1280]{2,1,0:T(8,128)}, u32[]{:S(2)}) copy-start(f32[2,64,1280]{2,1,0:T(8,128)} %param.18) | copy-start | bytes 1966084
  57.7 162.9 %all-gather.6.cloned.1.call-start = ((), (), s32[]{:S(2)}) async-start(), calls=%async_computation.6 | async-start | bytes 2949120 | tf_op jit(solution)/shard_map/all_gather | solution.py:21
  100.3 160.0 %all-gather.4.cloned.1.call-start = ((), (), s32[]{:S(2)}) async-start(), calls=%async_computation.4 | async-start | bytes 2949120 | tf_op jit(solution)/shard_map/all_gather | solution.py:21
  260.3 3.6 %copy-start.1 = (bf16[2,512,1280]{2,1,0:T(8,128)(2,1)S(1)}, bf16[2,512,1280]{2,1,0:T(8,128)(2,1)}, u32[]{:S(2)}) copy-start(bf16[2,512,1280]{2,1,0:T(8,128)(2,1)} %all-gather.6.cloned.1.call-done) | copy-start | bytes 7864324
  263.9 2.7 copy-start
Sparse Core Ops, SparseCore 0:
  10.4 44.8 reduce-scatter.7
  57.6 40.2 reduce-scatter.5
  100.2 40.2 reduce-scatter.3
  142.5 38.3 all-gather.7
  182.9 37.6 all-gather.5
  222.6 37.6 all-gather.3
where the time goes:
time: 275 us
  waiting for transfers between devices  245 us (89%)
  between operations  14.2 us (5%)
  local copies, waits for them, and re-layouts  7.76 us (3%)
  other arithmetic  7.18 us (3%)
    reduce_scatter x3, waiting for transfers between devices, step(): lax.psum_scatter(t[0], 'dp', scatter_dimension=1, tiled=True)  126 us
    all_gather x3, waiting for transfers between devices, step(): whole = [lax.all_gather(one[0], 'dp', axis=1, tiled=True) for one in new]  117 us
    unnamed x19, local copies, waits for them, and re-layouts  7.76 us
    convert_element_type x3, other arithmetic, adamw(): return ((w - 0.02 * step).astype(jnp.bfloat16), m, v)  7.18 us
  transfers between devices with their start and end apart: 6, of which 6 were waited for; matrix products, arithmetic and copies ran while one was open for 3% of the time, Pallas kernels for 0%

commit v1 on v0

v1 whole, which is shorter than its diff:
```python
import functools

import jax
import jax.numpy as jnp
from jax import lax
from jax.experimental import pallas as pl
from jax.experimental.pallas import tpu as pltpu
from jax.sharding import PartitionSpec as P

AXIS = "dp"
PARTS = 2


def adamw(w, m, v, g):
    m = 0.9 * m + 0.1 * g
    v = 0.95 * v + 0.05 * g * g
    step = m * lax.rsqrt(v + 1e-8) + 0.1 * w
    return (w - 0.02 * step).astype(jnp.bfloat16), m, v


def kernel(n, *refs):
    terms, weights, ms, vs = (refs[i : i + 3] for i in (0, 3, 6, 9))
    new_w, new_m, new_v = (refs[i : i + 3] for i in (12, 15, 18))
    held, sums, own = (refs[i : i + 3] for i in (21, 24, 27))
    held_sem, own_sem, m_sem, v_sem, sum_send, sum_recv, out_send, out_recv = refs[30:]
    layers = held[0].shape[0]
    me = lax.axis_index(AXIS)
    right, left = lax.rem(me + 1, n), lax.rem(me + n - 1, n)
    every = [(i, layer) for i in range(3) for layer in range(layers)]
    pieces = [
        (i, layer, part * (sums[i].shape[2] // PARTS), sums[i].shape[2] // PARTS)
        for i in range(3)
        for part in range(PARTS)
        for half in range(layers // 2)
        for layer in (half, half + layers // 2)
    ]

    def rightward(layer):
        return layer < layers // 2

    def to(layer):
        return {AXIS: right if rightward(layer) else left}

    def behind(layer, k):
        return lax.rem(me + n - k if rightward(layer) else me + k, n)

    def rows(i, block, first, count):
        return pl.ds(pl.multiple_of(block * sums[i].shape[2] + first, 16), count)

    def load(i, layer, k):
        block = rows(i, behind(layer, k), 0, sums[i].shape[2])
        return pltpu.make_async_copy(terms[i].at[0, layer, block], held[i].at[layer, block], held_sem.at[i, layer, k - 1])

    def sum_copy(at, step, source):
        i, layer, first, count = pieces[at]
        return pltpu.make_async_remote_copy(
            src_ref=source,
            dst_ref=sums[i].at[layer, step, pl.ds(first, count)],
            send_sem=sum_send.at[step, at],
            recv_sem=sum_recv.at[step, at],
            device_id=to(layer),
            device_id_type=pl.DeviceIdType.MESH,
        )

    def out_copy(at, step):
        i, layer, first, count = pieces[at]
        piece = new_w[i].at[layer, rows(i, behind(layer, step), first, count)]
        return pltpu.make_async_remote_copy(
            src_ref=piece,
            dst_ref=piece,
            send_sem=out_send.at[step, at],
            recv_sem=out_recv.at[step, at],
            device_id=to(layer),
            device_id_type=pl.DeviceIdType.MESH,
        )

    def landed(at, step):
        i, layer, first, count = pieces[at]
        return sums[i].at[layer, step, pl.ds(first, count)]

    def term(at, k):
        i, layer, first, count = pieces[at]
        return held[i].at[layer, rows(i, behind(layer, k), first, count)]

    def own_load(i, layer):
        return pltpu.make_async_copy(weights[i].at[layer, rows(i, me, 0, sums[i].shape[2])], own[i].at[layer], own_sem.at[i, layer])

    def moment_load(i):
        return (pltpu.make_async_copy(ms[i], new_m[i], m_sem.at[i]), pltpu.make_async_copy(vs[i], new_v[i], v_sem.at[i]))

    barrier = pltpu.get_barrier_semaphore()
    for neighbour in (left, right):
        pl.semaphore_signal(barrier, inc=1, device_id={AXIS: neighbour}, device_id_type=pl.DeviceIdType.MESH)
    for k in range(1, n + 1):
        for i, layer in every:
            load(i, layer, k).start()
    for i, layer in every:
        own_load(i, layer).start()
    for i in range(3):
        for copy in moment_load(i):
            copy.start()
    pl.semaphore_wait(barrier, 2)

    for at, (i, layer, first, count) in enumerate(pieces):
        if first == 0:
            load(i, layer, 1).wait()
        sum_copy(at, 0, term(at, 1)).start()

    @pl.loop(0, n - 2)
    def _(step):
        for at, (i, layer, first, count) in enumerate(pieces):
            here = landed(at, step)
            sum_copy(at, step, here).wait_recv()
            if first == 0:
                load(i, layer, step + 2).wait()
            here[...] = (here[...].astype(jnp.float32) + term(at, step + 2)[...].astype(jnp.float32)).astype(jnp.bfloat16)
            sum_copy(at, step + 1, here).start()

    for i, layer in every:
        own_load(i, layer).wait()
    for i in range(3):
        for copy in moment_load(i):
            copy.wait()

    for at, (i, layer, first, count) in enumerate(pieces):
        here = landed(at, n - 2)
        sum_copy(at, n - 2, here).wait_recv()
        if first == 0:
            load(i, layer, n).wait()
        g = (here[...].astype(jnp.float32) + term(at, n)[...].astype(jnp.float32)).astype(jnp.bfloat16).astype(jnp.float32)
        piece = (layer, pl.ds(first, count))
        w, m, v = adamw(own[i][piece].astype(jnp.float32), new_m[i][piece], new_v[i][piece], g)
        new_w[i][layer, rows(i, me, first, count)] = w
        new_m[i][piece] = m
        new_v[i][piece] = v
        out_copy(at, 0).start()

    @pl.loop(0, n - 2)
    def _(step):
        for at in range(len(pieces)):
            out_copy(at, step).wait_recv()
            out_copy(at, step + 1).start()

    for at in range(len(pieces)):
        out_copy(at, n - 2).wait_recv()

    @pl.loop(0, n - 1)
    def _(step):
        for at in range(len(pieces)):
            sum_copy(at, step, landed(at, step)).wait_send()
            out_copy(at, step).wait_send()


def put(*refs):
    count = len(refs) // 2
    copies = [pltpu.make_async_copy(refs[i], refs[count + i], refs[-1].at[i]) for i in range(count)]
    for copy in copies:
        copy.start()
    for copy in copies:
        copy.wait()


def solution(mesh):
    n = mesh.shape[AXIS]

    def step(*arrays):
        terms, weights, m, v = (arrays[i : i + 3] for i in (0, 3, 6, 9))
        layers = m[0].shape[0]
        count = 3 * layers * PARTS
        dma = pltpu.SemaphoreType.DMA
        arrays = [pltpu.with_memory_space_constraint(one, pltpu.HBM) for one in arrays]
        new = pl.pallas_call(
            functools.partial(kernel, n),
            out_shape=tuple(pltpu.VMEM(w.shape, w.dtype) for w in weights) + tuple(pltpu.VMEM(one.shape, one.dtype) for one in m + v),
            in_specs=[pl.BlockSpec(memory_space=pltpu.HBM)] * 12,
            out_specs=(pl.BlockSpec(memory_space=pltpu.VMEM),) * 9,
            scratch_shapes=[pltpu.VMEM(w.shape, w.dtype) for w in weights]
            + [pltpu.VMEM((layers, n - 1, *one.shape[1:]), w.dtype) for w, one in zip(weights, m, strict=True)]
            + [pltpu.VMEM(one.shape, w.dtype) for w, one in zip(weights, m, strict=True)]
            + [dma((3, layers, n)), dma((3, layers)), dma((3,)), dma((3,))]
            + [dma((n - 1, count))] * 4,
            compiler_params=pltpu.CompilerParams(collective_id=0, has_side_effects=True, vmem_limit_bytes=40 * 2**20),
        )(*arrays)
        new = [pltpu.with_memory_space_constraint(one, pltpu.VMEM) for one in new]
        return pl.pallas_call(
            put,
            out_shape=tuple(pltpu.HBM(one.shape, one.dtype) for one in new),
            in_specs=[pl.BlockSpec(memory_space=pltpu.VMEM)] * 9,
            out_specs=(pl.BlockSpec(memory_space=pltpu.HBM),) * 9,
            scratch_shapes=[dma((9,))],
            compiler_params=pltpu.CompilerParams(vmem_limit_bytes=2**20),
        )(*new)

    all_of, cut = P(None, None, None), P(None, AXIS, None)
    return jax.shard_map(
        step,
        mesh=mesh,
        in_specs=(P(("rep", AXIS), None, None, None),) * 3 + (all_of,) * 3 + (cut,) * 6,
        out_specs=(P("rep", None, None),) * 3 + (P("rep", AXIS, None),) * 6,
        check_vma=False,
    )
```

time: 275 us -> 166 us (0.60)
  waiting for transfers between devices: 245 us -> 0 us
  Pallas kernels: 0 us -> 165 us
  between operations: 14.2 us -> 0.65 us
  local copies, waits for them, and re-layouts: 7.76 us -> 0 us
  other arithmetic: 7.18 us -> 0 us
    pallas_call x0 -> x2, Pallas kernels: none -> 165 us  [the longest x1 160 us: step(): pl.pallas_call(functools.partial(kernel, n), out_shape=tuple((pltpu.VMEM(...]
    reduce_scatter x3 -> x0, waiting for transfers between devices: 126 us -> none  [step(): lax.psum_scatter(t[0], 'dp', scatter_dimension=1, tiled=True)]
    all_gather x3 -> x0, waiting for transfers between devices: 117 us -> none  [step(): whole = [lax.all_gather(one[0], 'dp', axis=1, tiled=True) for one in new]]
    unnamed x19 -> x0, local copies, waits for them, and re-layouts: 7.76 us -> none
    convert_element_type x3 -> x0, other arithmetic: 7.18 us -> none  [adamw(): return ((w - 0.02 * step).astype(jnp.bfloat16), m, v)]
  transfers between devices with their start and end apart: 6 -> 0, of which waited for: 6 -> 0; matrix products, arithmetic and copies ran while one was open for 3% -> 0% of each run, Pallas kernels for 0% -> 0%
where the time goes in v1:
time: 166 us; the launch traced here: 165 us
  Pallas kernels  165 us (99%)
    pallas_call x1, Pallas kernels, step(): pl.pallas_call(functools.partial(kernel, n), out_shape=tuple((pltpu.VMEM(...  160 us
    pallas_call x1, Pallas kernels, step(): pl.pallas_call(put, out_shape=tuple((pltpu.HBM(one.shape, one.dtype) for...  4.42 us

profile of v1, /device:TPU:22, one launch (start us, length us, event | category | flops | bytes accessed | tf_op | source)
XLA Modules:
  0.0 165.4 jit_solution(10257411575190388999)
XLA Ops:
  0.6 160.3 %shard_map.187 = (bf16[2,512,1280]{2,1,0:T(8,128)(2,1)S(1)}, bf16[2,512,1280]{2,1,0:T(8,128)(2,1)S(1)}, bf16[2,1280,512]{2,1,0:T(8,128)(2,1)S(1)}, f32[2,64,1280...) custom-call(bf16[1,2,512,1280]{3,2,1,0:T(8,128)(2,1)} %refs_0_.1, ...), custom_call_target="tpu_custom_call" | custom-call | tf_op jit(solution)/shard_map/pallas_call | solution.py:172
  161.0 4.4 %shard_map.188 = (bf16[2,512,1280]{2,1,0:T(8,128)(2,1)}, bf16[2,512,1280]{2,1,0:T(8,128)(2,1)}, bf16[2,1280,512]{2,1,0:T(8,128)(2,1)}, f32[2,64,1280]{2,1,0:T(8,...) custom-call(bf16[2,512,1280]{2,1,0:T(8,128)(2,1)S(1)} %get-tuple-ele, ...), custom_call_target="tpu_custom_call" | custom-call | tf_op jit(solution)/shard_map/pallas_call | solution.py:185

commit v2 on v1

--- a/solution.py
+++ b/solution.py
@@ -49,7 +49,7 @@
 
     def load(i, layer, k):
         block = rows(i, behind(layer, k), 0, sums[i].shape[2])
-        return pltpu.make_async_copy(terms[i].at[0, layer, block], held[i].at[layer, block], held_sem.at[i, layer, k - 1])
+        return pltpu.make_async_copy(terms[i].at[0, layer, block], held[i].at[layer, block], held_sem.at[i, layer, k - 2])
 
     def sum_copy(at, step, source):
         i, layer, first, count = pieces[at]
@@ -91,7 +91,12 @@
     barrier = pltpu.get_barrier_semaphore()
     for neighbour in (left, right):
         pl.semaphore_signal(barrier, inc=1, device_id={AXIS: neighbour}, device_id_type=pl.DeviceIdType.MESH)
-    for k in range(1, n + 1):
+    pl.semaphore_wait(barrier, 2)
+
+    for at, (i, layer, first, count) in enumerate(pieces):
+        sum_copy(at, 0, terms[i].at[0, layer, rows(i, behind(layer, 1), first, count)]).start()
+
+    for k in range(2, n + 1):
         for i, layer in every:
             load(i, layer, k).start()
     for i, layer in every:
@@ -99,12 +104,6 @@
     for i in range(3):
         for copy in moment_load(i):
             copy.start()
-    pl.semaphore_wait(barrier, 2)
-
-    for at, (i, layer, first, count) in enumerate(pieces):
-        if first == 0:
-            load(i, layer, 1).wait()
-        sum_copy(at, 0, term(at, 1)).start()
 
     @pl.loop(0, n - 2)
     def _(step):
@@ -140,20 +139,34 @@
         for at in range(len(pieces)):
             out_copy(at, step).wait_recv()
             out_copy(at, step + 1).start()
-
+        for at in range(len(pieces)):
+            sum_copy(at, step, landed(at, step)).wait_send()
+
+        @pl.when(step > 0)
+        def _():
+            for at in range(len(pieces)):
+                out_copy(at, step - 1).wait_send()
+
+    for at in range(len(pieces)):
+        sum_copy(at, n - 2, landed(at, n - 2)).wait_send()
+        out_copy(at, n - 3).wait_send()
     for at in range(len(pieces)):
         out_copy(at, n - 2).wait_recv()
-
-    @pl.loop(0, n - 1)
-    def _(step):
-        for at in range(len(pieces)):
-            sum_copy(at, step, landed(at, step)).wait_send()
-            out_copy(at, step).wait_send()
+    for at in range(len(pieces)):
+        out_copy(at, n - 2).wait_send()
 
 
 def put(*refs):
     count = len(refs) // 2
-    copies = [pltpu.make_async_copy(refs[i], refs[count + i], refs[-1].at[i]) for i in range(count)]
+    halves = [(i, half) for i in range(count) for half in range(2)]
+    copies = [
+        pltpu.make_async_copy(
+            refs[i].at[pl.ds(half * (refs[i].shape[0] // 2), refs[i].shape[0] // 2)],
+            refs[count + i].at[pl.ds(half * (refs[i].shape[0] // 2), refs[i].shape[0] // 2)],
+            refs[-1].at[i, half],
+        )
+        for i, half in halves
+    ]
     for copy in copies:
         copy.start()
     for copy in copies:
@@ -177,7 +190,7 @@
             scratch_shapes=[pltpu.VMEM(w.shape, w.dtype) for w in weights]
             + [pltpu.VMEM((layers, n - 1, *one.shape[1:]), w.dtype) for w, one in zip(weights, m, strict=True)]
             + [pltpu.VMEM(one.shape, w.dtype) for w, one in zip(weights, m, strict=True)]
-            + [dma((3, layers, n)), dma((3, layers)), dma((3,)), dma((3,))]
+            + [dma((3, layers, n - 1)), dma((3, layers)), dma((3,)), dma((3,))]
             + [dma((n - 1, count))] * 4,
             compiler_params=pltpu.CompilerParams(collective_id=0, has_side_effects=True, vmem_limit_bytes=40 * 2**20),
         )(*arrays)
@@ -187,7 +200,7 @@
             out_shape=tuple(pltpu.HBM(one.shape, one.dtype) for one in new),
             in_specs=[pl.BlockSpec(memory_space=pltpu.VMEM)] * 9,
             out_specs=(pl.BlockSpec(memory_space=pltpu.HBM),) * 9,
-            scratch_shapes=[dma((9,))],
+            scratch_shapes=[dma((9, 2))],
             compiler_params=pltpu.CompilerParams(vmem_limit_bytes=2**20),
         )(*new)
 

time: 166 us -> 165 us (level)
  no operation moved by 1% of the time
where the time goes in v2:
time: 165 us
  Pallas kernels  164 us (99%)
    pallas_call x1, Pallas kernels, step(): pl.pallas_call(functools.partial(kernel, n), out_shape=tuple((pltpu.VMEM(...  160 us
    pallas_call x1, Pallas kernels, step(): pl.pallas_call(put, out_shape=tuple((pltpu.HBM(one.shape, one.dtype) for...  4.49 us

profile of v2, /device:TPU:22, one launch (start us, length us, event | category | flops | bytes accessed | tf_op | source)
XLA Modules:
  0.0 164.8 jit_solution(15822858294240262287)
XLA Ops:
  0.6 159.6 %shard_map.187 = (bf16[2,512,1280]{2,1,0:T(8,128)(2,1)S(1)}, bf16[2,512,1280]{2,1,0:T(8,128)(2,1)S(1)}, bf16[2,1280,512]{2,1,0:T(8,128)(2,1)S(1)}, f32[2,64,1280...) custom-call(bf16[1,2,512,1280]{3,2,1,0:T(8,128)(2,1)} %refs_0_.1, ...), custom_call_target="tpu_custom_call" | custom-call | tf_op jit(solution)/shard_map/pallas_call | solution.py:185
  160.3 4.5 %shard_map.188 = (bf16[2,512,1280]{2,1,0:T(8,128)(2,1)}, bf16[2,512,1280]{2,1,0:T(8,128)(2,1)}, bf16[2,1280,512]{2,1,0:T(8,128)(2,1)}, f32[2,64,1280]{2,1,0:T(8,...) custom-call(bf16[2,512,1280]{2,1,0:T(8,128)(2,1)S(1)} %get-tuple-ele, ...), custom_call_target="tpu_custom_call" | custom-call | tf_op jit(solution)/shard_map/pallas_call | solution.py:198

commit v3 on v2

--- a/solution.py
+++ b/solution.py
@@ -22,7 +22,7 @@
     terms, weights, ms, vs = (refs[i : i + 3] for i in (0, 3, 6, 9))
     new_w, new_m, new_v = (refs[i : i + 3] for i in (12, 15, 18))
     held, sums, own = (refs[i : i + 3] for i in (21, 24, 27))
-    held_sem, own_sem, m_sem, v_sem, sum_send, sum_recv, out_send, out_recv = refs[30:]
+    first_sem, held_sem, own_sem, m_sem, v_sem, sum_send, sum_recv, out_send, out_recv = refs[30:]
     layers = held[0].shape[0]
     me = lax.axis_index(AXIS)
     right, left = lax.rem(me + 1, n), lax.rem(me + n - 1, n)
@@ -82,6 +82,10 @@
         i, layer, first, count = pieces[at]
         return held[i].at[layer, rows(i, behind(layer, k), first, count)]
 
+    def first_load(at):
+        i, layer, first, count = pieces[at]
+        return pltpu.make_async_copy(terms[i].at[0, layer, rows(i, behind(layer, 1), first, count)], term(at, 1), first_sem.at[at])
+
     def own_load(i, layer):
         return pltpu.make_async_copy(weights[i].at[layer, rows(i, me, 0, sums[i].shape[2])], own[i].at[layer], own_sem.at[i, layer])
 
@@ -91,10 +95,13 @@
     barrier = pltpu.get_barrier_semaphore()
     for neighbour in (left, right):
         pl.semaphore_signal(barrier, inc=1, device_id={AXIS: neighbour}, device_id_type=pl.DeviceIdType.MESH)
+    for at in range(len(pieces)):
+        first_load(at).start()
     pl.semaphore_wait(barrier, 2)
 
-    for at, (i, layer, first, count) in enumerate(pieces):
-        sum_copy(at, 0, terms[i].at[0, layer, rows(i, behind(layer, 1), first, count)]).start()
+    for at in range(len(pieces)):
+        first_load(at).wait()
+        sum_copy(at, 0, term(at, 1)).start()
 
     for k in range(2, n + 1):
         for i, layer in every:
@@ -158,15 +165,7 @@
 
 def put(*refs):
     count = len(refs) // 2
-    halves = [(i, half) for i in range(count) for half in range(2)]
-    copies = [
-        pltpu.make_async_copy(
-            refs[i].at[pl.ds(half * (refs[i].shape[0] // 2), refs[i].shape[0] // 2)],
-            refs[count + i].at[pl.ds(half * (refs[i].shape[0] // 2), refs[i].shape[0] // 2)],
-            refs[-1].at[i, half],
-        )
-        for i, half in halves
-    ]
+    copies = [pltpu.make_async_copy(refs[i], refs[count + i], refs[-1].at[i]) for i in range(count)]
     for copy in copies:
         copy.start()
     for copy in copies:
@@ -190,7 +189,7 @@
             scratch_shapes=[pltpu.VMEM(w.shape, w.dtype) for w in weights]
             + [pltpu.VMEM((layers, n - 1, *one.shape[1:]), w.dtype) for w, one in zip(weights, m, strict=True)]
             + [pltpu.VMEM(one.shape, w.dtype) for w, one in zip(weights, m, strict=True)]
-            + [dma((3, layers, n - 1)), dma((3, layers)), dma((3,)), dma((3,))]
+            + [dma((count,)), dma((3, layers, n - 1)), dma((3, layers)), dma((3,)), dma((3,))]
             + [dma((n - 1, count))] * 4,
             compiler_params=pltpu.CompilerParams(collective_id=0, has_side_effects=True, vmem_limit_bytes=40 * 2**20),
         )(*arrays)
@@ -200,7 +199,7 @@
             out_shape=tuple(pltpu.HBM(one.shape, one.dtype) for one in new),
             in_specs=[pl.BlockSpec(memory_space=pltpu.VMEM)] * 9,
             out_specs=(pl.BlockSpec(memory_space=pltpu.HBM),) * 9,
-            scratch_shapes=[dma((9, 2))],
+            scratch_shapes=[dma((9,))],
             compiler_params=pltpu.CompilerParams(vmem_limit_bytes=2**20),
         )(*new)
 

time: 165 us -> 166 us (level)
  no operation moved by 1% of the time
where the time goes in v3:
time: 166 us; the launch traced here: 165 us
  Pallas kernels  165 us (99%)
    pallas_call x1, Pallas kernels, step(): pl.pallas_call(functools.partial(kernel, n), out_shape=tuple((pltpu.VMEM(...  160 us
    pallas_call x1, Pallas kernels, step(): pl.pallas_call(put, out_shape=tuple((pltpu.HBM(one.shape, one.dtype) for...  4.42 us

profile of v3, /device:TPU:22, one launch (start us, length us, event | category | flops | bytes accessed | tf_op | source)
XLA Modules:
  0.0 165.2 jit_solution(3459800315391500106)
XLA Ops:
  0.6 160.1 %shard_map.187 = (bf16[2,512,1280]{2,1,0:T(8,128)(2,1)S(1)}, bf16[2,512,1280]{2,1,0:T(8,128)(2,1)S(1)}, bf16[2,1280,512]{2,1,0:T(8,128)(2,1)S(1)}, f32[2,64,1280...) custom-call(bf16[1,2,512,1280]{3,2,1,0:T(8,128)(2,1)} %refs_0_.1, ...), custom_call_target="tpu_custom_call" | custom-call | tf_op jit(solution)/shard_map/pallas_call | solution.py:184
  160.7 4.4 %shard_map.188 = (bf16[2,512,1280]{2,1,0:T(8,128)(2,1)}, bf16[2,512,1280]{2,1,0:T(8,128)(2,1)}, bf16[2,1280,512]{2,1,0:T(8,128)(2,1)}, f32[2,64,1280]{2,1,0:T(8,...) custom-call(bf16[2,512,1280]{2,1,0:T(8,128)(2,1)S(1)} %get-tuple-ele, ...), custom_call_target="tpu_custom_call" | custom-call | tf_op jit(solution)/shard_map/pallas_call | solution.py:197

commit v4 on v2

--- a/solution.py
+++ b/solution.py
@@ -8,7 +8,7 @@
 from jax.sharding import PartitionSpec as P
 
 AXIS = "dp"
-PARTS = 2
+PARTS = 1
 
 
 def adamw(w, m, v, g):
@@ -16,6 +16,11 @@
     v = 0.95 * v + 0.05 * g * g
     step = m * lax.rsqrt(v + 1e-8) + 0.1 * w
     return (w - 0.02 * step).astype(jnp.bfloat16), m, v
+
+
+def cut(rows):
+    edges = [16 * (rows // 16 * part // PARTS) for part in range(PARTS)] + [rows]
+    return [(a, b - a) for a, b in zip(edges, edges[1:])]
 
 
 def kernel(n, *refs):
@@ -28,7 +33,7 @@
     right, left = lax.rem(me + 1, n), lax.rem(me + n - 1, n)
     every = [(i, layer) for i in range(3) for layer in range(layers)]
     pieces = [
-        (i, layer, part * (sums[i].shape[2] // PARTS), sums[i].shape[2] // PARTS)
+        (i, layer, *cut(sums[i].shape[2])[part])
         for i in range(3)
         for part in range(PARTS)
         for half in range(layers // 2)
@@ -158,15 +163,7 @@
 
 def put(*refs):
     count = len(refs) // 2
-    halves = [(i, half) for i in range(count) for half in range(2)]
-    copies = [
-        pltpu.make_async_copy(
-            refs[i].at[pl.ds(half * (refs[i].shape[0] // 2), refs[i].shape[0] // 2)],
-            refs[count + i].at[pl.ds(half * (refs[i].shape[0] // 2), refs[i].shape[0] // 2)],
-            refs[-1].at[i, half],
-        )
-        for i, half in halves
-    ]
+    copies = [pltpu.make_async_copy(refs[i], refs[count + i], refs[-1].at[i]) for i in range(count)]
     for copy in copies:
         copy.start()
     for copy in copies:
@@ -200,15 +197,15 @@
             out_shape=tuple(pltpu.HBM(one.shape, one.dtype) for one in new),
             in_specs=[pl.BlockSpec(memory_space=pltpu.VMEM)] * 9,
             out_specs=(pl.BlockSpec(memory_space=pltpu.HBM),) * 9,
-            scratch_shapes=[dma((9, 2))],
+            scratch_shapes=[dma((9,))],
             compiler_params=pltpu.CompilerParams(vmem_limit_bytes=2**20),
         )(*new)
 
-    all_of, cut = P(None, None, None), P(None, AXIS, None)
+    all_of, part = P(None, None, None), P(None, AXIS, None)
     return jax.shard_map(
         step,
         mesh=mesh,
-        in_specs=(P(("rep", AXIS), None, None, None),) * 3 + (all_of,) * 3 + (cut,) * 6,
+        in_specs=(P(("rep", AXIS), None, None, None),) * 3 + (all_of,) * 3 + (part,) * 6,
         out_specs=(P("rep", None, None),) * 3 + (P("rep", AXIS, None),) * 6,
         check_vma=False,
     )

time: 165 us -> 163 us (0.988)
  no operation moved by 1% of the time
where the time goes in v4:
time: 163 us
  Pallas kernels  163 us (100%)
    pallas_call x1, Pallas kernels, step(): pl.pallas_call(functools.partial(kernel, n), out_shape=tuple((pltpu.VMEM(...  158 us
    pallas_call x1, Pallas kernels, step(): pl.pallas_call(put, out_shape=tuple((pltpu.HBM(one.shape, one.dtype) for...  4.42 us

profile of v4, /device:TPU:22, one launch (start us, length us, event | category | flops | bytes accessed | tf_op | source)
XLA Modules:
  0.0 163.2 jit_solution(12767153190909027995)
XLA Ops:
  0.6 158.1 %shard_map.187 = (bf16[2,512,1280]{2,1,0:T(8,128)(2,1)S(1)}, bf16[2,512,1280]{2,1,0:T(8,128)(2,1)S(1)}, bf16[2,1280,512]{2,1,0:T(8,128)(2,1)S(1)}, f32[2,64,1280...) custom-call(bf16[1,2,512,1280]{3,2,1,0:T(8,128)(2,1)} %refs_0_.1, ...), custom_call_target="tpu_custom_call" | custom-call | tf_op jit(solution)/shard_map/pallas_call | solution.py:182
  158.8 4.4 %shard_map.188 = (bf16[2,512,1280]{2,1,0:T(8,128)(2,1)}, bf16[2,512,1280]{2,1,0:T(8,128)(2,1)}, bf16[2,1280,512]{2,1,0:T(8,128)(2,1)}, f32[2,64,1280]{2,1,0:T(8,...) custom-call(bf16[2,512,1280]{2,1,0:T(8,128)(2,1)S(1)} %get-tuple-ele, ...), custom_call_target="tpu_custom_call" | custom-call | tf_op jit(solution)/shard_map/pallas_call | solution.py:195

commit v5 on v4

--- a/solution.py
+++ b/solution.py
@@ -27,7 +27,7 @@
     terms, weights, ms, vs = (refs[i : i + 3] for i in (0, 3, 6, 9))
     new_w, new_m, new_v = (refs[i : i + 3] for i in (12, 15, 18))
     held, sums, own = (refs[i : i + 3] for i in (21, 24, 27))
-    held_sem, own_sem, m_sem, v_sem, sum_send, sum_recv, out_send, out_recv = refs[30:]
+    entered, held_sem, own_sem, m_sem, v_sem, sum_send, sum_recv, out_send, out_recv = refs[30:]
     layers = held[0].shape[0]
     me = lax.axis_index(AXIS)
     right, left = lax.rem(me + 1, n), lax.rem(me + n - 1, n)
@@ -94,12 +94,15 @@
         return (pltpu.make_async_copy(ms[i], new_m[i], m_sem.at[i]), pltpu.make_async_copy(vs[i], new_v[i], v_sem.at[i]))
 
     barrier = pltpu.get_barrier_semaphore()
-    for neighbour in (left, right):
-        pl.semaphore_signal(barrier, inc=1, device_id={AXIS: neighbour}, device_id_type=pl.DeviceIdType.MESH)
-    pl.semaphore_wait(barrier, 2)
-
-    for at, (i, layer, first, count) in enumerate(pieces):
-        sum_copy(at, 0, terms[i].at[0, layer, rows(i, behind(layer, 1), first, count)]).start()
+    pl.semaphore_signal(barrier, inc=1, device_id={AXIS: left}, device_id_type=pl.DeviceIdType.MESH)
+    pl.semaphore_wait(barrier, 1)
+    pl.semaphore_signal(entered, inc=1, device_id={AXIS: right}, device_id_type=pl.DeviceIdType.MESH)
+    for rightbound in (True, False):
+        if not rightbound:
+            pl.semaphore_wait(entered, 1)
+        for at, (i, layer, first, count) in enumerate(pieces):
+            if rightward(layer) == rightbound:
+                sum_copy(at, 0, terms[i].at[0, layer, rows(i, behind(layer, 1), first, count)]).start()
 
     for k in range(2, n + 1):
         for i, layer in every:
@@ -187,7 +190,7 @@
             scratch_shapes=[pltpu.VMEM(w.shape, w.dtype) for w in weights]
             + [pltpu.VMEM((layers, n - 1, *one.shape[1:]), w.dtype) for w, one in zip(weights, m, strict=True)]
             + [pltpu.VMEM(one.shape, w.dtype) for w, one in zip(weights, m, strict=True)]
-            + [dma((3, layers, n - 1)), dma((3, layers)), dma((3,)), dma((3,))]
+            + [pltpu.SemaphoreType.REGULAR, dma((3, layers, n - 1)), dma((3, layers)), dma((3,)), dma((3,))]
             + [dma((n - 1, count))] * 4,
             compiler_params=pltpu.CompilerParams(collective_id=0, has_side_effects=True, vmem_limit_bytes=40 * 2**20),
         )(*arrays)

time: 163 us -> 163 us (level)
  no operation moved by 1% of the time
where the time goes in v5:
time: 163 us
  Pallas kernels  162 us (99%)
    pallas_call x1, Pallas kernels, step(): pl.pallas_call(functools.partial(kernel, n), out_shape=tuple((pltpu.VMEM(...  158 us
    pallas_call x1, Pallas kernels, step(): pl.pallas_call(put, out_shape=tuple((pltpu.HBM(one.shape, one.dtype) for...  4.42 us

profile of v5, /device:TPU:22, one launch (start us, length us, event | category | flops | bytes accessed | tf_op | source)
XLA Modules:
  0.0 162.7 jit_solution(1639375385301415143)
XLA Ops:
  0.6 157.6 %shard_map.187 = (bf16[2,512,1280]{2,1,0:T(8,128)(2,1)S(1)}, bf16[2,512,1280]{2,1,0:T(8,128)(2,1)S(1)}, bf16[2,1280,512]{2,1,0:T(8,128)(2,1)S(1)}, f32[2,64,1280...) custom-call(bf16[1,2,512,1280]{3,2,1,0:T(8,128)(2,1)} %refs_0_.1, ...), custom_call_target="tpu_custom_call" | custom-call | tf_op jit(solution)/shard_map/pallas_call | solution.py:185
  158.3 4.4 %shard_map.188 = (bf16[2,512,1280]{2,1,0:T(8,128)(2,1)}, bf16[2,512,1280]{2,1,0:T(8,128)(2,1)}, bf16[2,1280,512]{2,1,0:T(8,128)(2,1)}, f32[2,64,1280]{2,1,0:T(8,...) custom-call(bf16[2,512,1280]{2,1,0:T(8,128)(2,1)S(1)} %get-tuple-ele, ...), custom_call_target="tpu_custom_call" | custom-call | tf_op jit(solution)/shard_map/pallas_call | solution.py:198

commit v6 on v0

v6 whole, which is shorter than its diff:
```python
import functools

import jax
import jax.numpy as jnp
from jax import lax
from jax.experimental import pallas as pl
from jax.experimental.pallas import tpu as pltpu
from jax.sharding import PartitionSpec as P

AXIS = "dp"
MESH = pl.DeviceIdType.MESH


def adamw(w, m, v, g):
    m = 0.9 * m + 0.1 * g
    v = 0.95 * v + 0.05 * g * g
    step = m * lax.rsqrt(v + 1e-8) + 0.1 * w
    return (w - 0.02 * step).astype(jnp.bfloat16), m, v


def stacks_of(moments):
    by_shape = {}
    for i, one in enumerate(moments):
        by_shape.setdefault(one.shape, []).append(i)
    return list(by_shape.values())


def kernel(n, stacks, *refs):
    terms, weights, ms, vs = (refs[i : i + 3] for i in (0, 3, 6, 9))
    k = len(stacks)
    new_w, new_m, new_v = refs[12 : 12 + k], refs[12 + k : 15 + k], refs[15 + k : 18 + k]
    held, own, sums = refs[18 + k : 21 + k], refs[21 + k : 24 + k], refs[24 + k : 24 + 2 * k]
    entered, held_sem, own_sem, m_sem, v_sem, first_send, first_recv, sum_send, sum_recv, out_send, out_recv = refs[24 + 2 * k :]
    layers, block = own[0].shape[0], [one.shape[1] for one in own]
    me = lax.axis_index(AXIS)
    right, left = lax.rem(me + 1, n), lax.rem(me + n - 1, n)
    turns = [layer for half in range(layers // 2) for layer in (half, half + layers // 2)]
    every = [(i, layer) for stack in stacks for layer in turns for i in stack]
    loads = [(s, layer) for s in range(k) for layer in turns]

    def rightward(layer):
        return layer < layers // 2

    def behind(layer, steps):
        return lax.rem(me + n - steps if rightward(layer) else me + steps, n)

    def rows(i, device):
        return pl.ds(pl.multiple_of(device * block[i], 16), block[i])

    def send(layer, source, target, send_sem, recv_sem):
        return pltpu.make_async_remote_copy(
            src_ref=source,
            dst_ref=target,
            send_sem=send_sem,
            recv_sem=recv_sem,
            device_id={AXIS: right if rightward(layer) else left},
            device_id_type=MESH,
        )

    def first_copy(i, layer):
        s, place = next((s, stack.index(i)) for s, stack in enumerate(stacks) if i in stack)
        source = terms[i].at[0, layer, rows(i, behind(layer, 1))]
        return send(layer, source, sums[s].at[layer, 0, place], first_send.at[i, layer], first_recv.at[i, layer])

    def sum_copy(s, layer, step):
        return send(layer, sums[s].at[layer, step - 1], sums[s].at[layer, step], sum_send.at[step - 1, s, layer], sum_recv.at[step - 1, s, layer])

    def out_copy(s, layer, step):
        piece = new_w[s].at[layer, behind(layer, step)]
        return send(layer, piece, piece, out_send.at[step, s, layer], out_recv.at[step, s, layer])

    def load(i, layer, steps):
        part = rows(i, behind(layer, steps))
        return pltpu.make_async_copy(terms[i].at[0, layer, part], held[i].at[layer, part], held_sem.at[i, layer, steps - 2])

    def own_load(i):
        return pltpu.make_async_copy(weights[i].at[:, rows(i, me)], own[i], own_sem.at[i])

    def moment_load(i):
        return (pltpu.make_async_copy(ms[i], new_m[i], m_sem.at[i]), pltpu.make_async_copy(vs[i], new_v[i], v_sem.at[i]))

    def total(s, layer, step, place):
        i = stacks[s][place]
        load(i, layer, step + 2).wait()
        term = held[i][layer, rows(i, behind(layer, step + 2)), :]
        return (sums[s][layer, step, place].astype(jnp.float32) + term.astype(jnp.float32)).astype(jnp.bfloat16)

    barrier = pltpu.get_barrier_semaphore()
    pl.semaphore_signal(barrier, inc=1, device_id={AXIS: left}, device_id_type=MESH)
    pl.semaphore_wait(barrier, 1)
    pl.semaphore_signal(entered, inc=1, device_id={AXIS: right}, device_id_type=MESH)
    for i, layer in every:
        if rightward(layer):
            first_copy(i, layer).start()
    pl.semaphore_wait(entered, 1)
    for i, layer in every:
        if not rightward(layer):
            first_copy(i, layer).start()

    for steps in range(2, n + 1):
        for i, layer in every:
            load(i, layer, steps).start()
    for i in range(3):
        own_load(i).start()
        for copy in moment_load(i):
            copy.start()

    def add_and_send(s, layer, step):
        for place in range(len(stacks[s])):
            sums[s][layer, step, place] = total(s, layer, step, place)
        sum_copy(s, layer, step + 1).start()

    for s, layer in loads:
        for i in stacks[s]:
            first_copy(i, layer).wait_recv()
        add_and_send(s, layer, 0)

    @pl.loop(1, n - 2)
    def _(step):
        for s, layer in loads:
            sum_copy(s, layer, step).wait_recv()
            add_and_send(s, layer, step)

    for i in range(3):
        own_load(i).wait()
        for copy in moment_load(i):
            copy.wait()

    for s, layer in loads:
        sum_copy(s, layer, n - 2).wait_recv()
        for place, i in enumerate(stacks[s]):
            g = total(s, layer, n - 2, place).astype(jnp.float32)
            w, m, v = adamw(own[i][layer].astype(jnp.float32), new_m[i][layer], new_v[i][layer], g)
            new_w[s][layer, me, place] = w
            new_m[i][layer] = m
            new_v[i][layer] = v
        out_copy(s, layer, 0).start()

    for i, layer in every:
        first_copy(i, layer).wait_send()

    @pl.loop(0, n - 2)
    def _(step):
        for s, layer in loads:
            out_copy(s, layer, step).wait_recv()
            out_copy(s, layer, step + 1).start()
        for s, layer in loads:
            sum_copy(s, layer, step + 1).wait_send()

        @pl.when(step > 0)
        def _():
            for s, layer in loads:
                out_copy(s, layer, step - 1).wait_send()

    for s, layer in loads:
        out_copy(s, layer, n - 3).wait_send()
    for s, layer in loads:
        out_copy(s, layer, n - 2).wait_recv()
    for s, layer in loads:
        out_copy(s, layer, n - 2).wait_send()


def put(stacks, *refs):
    stacked, moments = refs[: len(stacks)], refs[len(stacks) : len(stacks) + 6]
    outs, sem = refs[len(stacks) + 6 : -1], refs[-1]
    sources = list(moments)
    for i in reversed(range(3)):
        s, place = next((s, stack.index(i)) for s, stack in enumerate(stacks) if i in stack)
        sources.insert(0, stacked[s].at[:, :, place])
    copies = [pltpu.make_async_copy(source, out, sem.at[i]) for i, (source, out) in enumerate(zip(sources, outs, strict=True))]
    for copy in copies:
        copy.start()
    for copy in copies:
        copy.wait()


def solution(mesh):
    n = mesh.shape[AXIS]

    def step(*arrays):
        terms, weights, m, v = (arrays[i : i + 3] for i in (0, 3, 6, 9))
        layers = m[0].shape[0]
        stacks = stacks_of(m)
        dma = pltpu.SemaphoreType.DMA
        stack_shapes = [(len(stack), *m[stack[0]].shape[1:]) for stack in stacks]
        arrays = [pltpu.with_memory_space_constraint(one, pltpu.HBM) for one in arrays]
        new = pl.pallas_call(
            functools.partial(kernel, n, stacks),
            out_shape=tuple(pltpu.VMEM((layers, n, *shape), weights[0].dtype) for shape in stack_shapes)
            + tuple(pltpu.VMEM(one.shape, one.dtype) for one in m + v),
            in_specs=[pl.BlockSpec(memory_space=pltpu.HBM)] * 12,
            out_specs=(pl.BlockSpec(memory_space=pltpu.VMEM),) * (6 + len(stacks)),
            scratch_shapes=[pltpu.VMEM(w.shape, w.dtype) for w in weights]
            + [pltpu.VMEM(one.shape, w.dtype) for w, one in zip(weights, m, strict=True)]
            + [pltpu.VMEM((layers, n - 1, *shape), weights[0].dtype) for shape in stack_shapes]
            + [pltpu.SemaphoreType.REGULAR, dma((3, layers, n - 1)), dma((3,)), dma((3,)), dma((3,))]
            + [dma((3, layers))] * 2
            + [dma((n - 2, len(stacks), layers))] * 2
            + [dma((n - 1, len(stacks), layers))] * 2,
            compiler_params=pltpu.CompilerParams(collective_id=0, has_side_effects=True, vmem_limit_bytes=40 * 2**20),
        )(*arrays)
        new = [pltpu.with_memory_space_constraint(one, pltpu.VMEM) for one in new]
        outs = pl.pallas_call(
            functools.partial(put, stacks),
            out_shape=tuple(pltpu.HBM((layers, n, *one.shape[1:]), w.dtype) for w, one in zip(weights, m, strict=True))
            + tuple(pltpu.HBM(one.shape, one.dtype) for one in m + v),
            in_specs=[pl.BlockSpec(memory_space=pltpu.VMEM)] * (6 + len(stacks)),
            out_specs=(pl.BlockSpec(memory_space=pltpu.HBM),) * 9,
            scratch_shapes=[dma((9,))],
            compiler_params=pltpu.CompilerParams(vmem_limit_bytes=2**20),
        )(*new)
        return (*(out.reshape(w.shape) for out, w in zip(outs[:3], weights, strict=True)), *outs[3:])

    all_of, part = P(None, None, None), P(None, AXIS, None)
    return jax.shard_map(
        step,
        mesh=mesh,
        in_specs=(P(("rep", AXIS), None, None, None),) * 3 + (all_of,) * 3 + (part,) * 6,
        out_specs=(P("rep", None, None),) * 3 + (P("rep", AXIS, None),) * 6,
        check_vma=False,
    )
```

time: 275 us -> 162 us (0.59)
  waiting for transfers between devices: 245 us -> 0 us
  Pallas kernels: 0 us -> 162 us
  between operations: 14.2 us -> 0.65 us
  local copies, waits for them, and re-layouts: 7.76 us -> 0 us
  other arithmetic: 7.18 us -> 0 us
    pallas_call x0 -> x2, Pallas kernels: none -> 162 us  [the longest x1 157 us: step(): pl.pallas_call(functools.partial(kernel, n, stacks), out_shape=tuple((plt...]
    reduce_scatter x3 -> x0, waiting for transfers between devices: 126 us -> none  [step(): lax.psum_scatter(t[0], 'dp', scatter_dimension=1, tiled=True)]
    all_gather x3 -> x0, waiting for transfers between devices: 117 us -> none  [step(): whole = [lax.all_gather(one[0], 'dp', axis=1, tiled=True) for one in new]]
    unnamed x19 -> x0, local copies, waits for them, and re-layouts: 7.76 us -> none
    convert_element_type x3 -> x0, other arithmetic: 7.18 us -> none  [adamw(): return ((w - 0.02 * step).astype(jnp.bfloat16), m, v)]
  transfers between devices with their start and end apart: 6 -> 0, of which waited for: 6 -> 0; matrix products, arithmetic and copies ran while one was open for 3% -> 0% of each run, Pallas kernels for 0% -> 0%
where the time goes in v6:
time: 162 us
  Pallas kernels  162 us (100%)
    pallas_call x1, Pallas kernels, step(): pl.pallas_call(functools.partial(kernel, n, stacks), out_shape=tuple((plt...  157 us
    pallas_call x1, Pallas kernels, step(): pl.pallas_call(functools.partial(put, stacks), out_shape=tuple((pltpu.HBM...  4.42 us

profile of v6, /device:TPU:22, one launch (start us, length us, event | category | flops | bytes accessed | tf_op | source)
XLA Modules:
  0.0 162.2 jit_solution(17187838802404921989)
XLA Ops:
  0.6 157.1 %shard_map.187 = (bf16[2,8,2,64,1280]{4,3,2,1,0:T(8,128)(2,1)S(1)}, bf16[2,8,1,160,512]{4,3,2,1,0:T(8,128)(2,1)S(1)}, f32[2,64,1280]{2,1,0:T(8,128)S(1)}, f32[2,...) custom-call(bf16[1,2,512,1280]{3,2,1,0:T(8,128)(2,1)} %refs_0_.1, ...), custom_call_target="tpu_custom_call" | custom-call | tf_op jit(solution)/shard_map/pallas_call | solution.py:187
  157.8 4.4 %shard_map.188 = (bf16[2,8,64,1280]{3,2,1,0:T(8,128)(2,1)}, bf16[2,8,64,1280]{3,2,1,0:T(8,128)(2,1)}, bf16[2,8,160,512]{3,2,1,0:T(8,128)(2,1)}, f32[2,64,1280]{2...) custom-call(bf16[2,8,2,64,1280]{4,3,2,1,0:T(8,128)(2,1)S(1)} %get-tu, ...), custom_call_target="tpu_custom_call" | custom-call | tf_op jit(solution)/shard_map/pallas_call | solution.py:203

commit v7 on v0

v7 whole, which is shorter than its diff:
```python
import functools

import jax
import jax.numpy as jnp
from jax import lax
from jax.experimental import pallas as pl
from jax.experimental.pallas import tpu as pltpu
from jax.sharding import PartitionSpec as P

AXIS = "dp"
MESH = pl.DeviceIdType.MESH
ROWS, LANES = 16, 128
MOVED = 1


def adamw(w, m, v, g):
    m = 0.9 * m + 0.1 * g
    v = 0.95 * v + 0.05 * g * g
    step = m * lax.rsqrt(v + 1e-8) + 0.1 * w
    return (w - 0.02 * step).astype(jnp.bfloat16), m, v


class Plan:
    def __init__(self, shapes):
        self.layers = shapes[0][0]
        self.block = [shape[1] for shape in shapes]
        self.wide = [shape[2] // LANES for shape in shapes]
        half = self.layers // 2
        order = sorted(range(len(shapes)), key=lambda i: (self.wide[i], i))
        bands, tile = {}, 0
        for rightward in (False, True):
            bands[rightward] = []
            for layer in range(half) if rightward else range(half, self.layers):
                for i in order:
                    for row in range(self.block[i] // ROWS):
                        bands[rightward].append((layer, i, row, tile))
                        tile += self.wide[i]
        self.tiles = tile
        self.sums = self.cut(bands[False], bands[True])
        self.news = self.cut(bands[False] + bands[True][:MOVED], bands[True][MOVED:])

    def cut(self, left, right):
        copies = []
        for rightward, bands in ((True, right), (False, left)):
            count = sum(self.wide[i] for _, i, _, _ in bands)
            at = next(k for k, band in enumerate(bands) if 2 * (band[3] - bands[0][3]) >= count - self.wide[band[1]])
            copies.append([(rightward, part) for part in (bands[:at], bands[at:])])
        return [
            (rightward, part[0][3], sum(self.wide[i] for _, i, _, _ in part), self.runs(part))
            for pair in zip(*copies)
            for rightward, part in pair
        ]

    def runs(self, bands):
        runs = []
        for layer, i, row, tile in bands:
            if runs and runs[-1][:2] == [layer, i]:
                runs[-1][3] += 1
            else:
                runs.append([layer, i, row, 1, tile])
        return runs


def kernel(n, plan, *refs):
    terms, weights, ms, vs = (refs[i : i + 3] for i in (0, 3, 6, 9))
    new_w, new_m, new_v, held, own, first = (refs[i : i + 3] for i in (12, 15, 18, 21, 24, 27))
    sums, news, entered, held_sem, own_sem, m_sem, v_sem, first_send, first_recv, sum_send, sum_recv, out_send, out_recv = refs[30:]
    me = lax.axis_index(AXIS)
    right, left = lax.rem(me + 1, n), lax.rem(me + n - 1, n)
    half = plan.layers // 2
    every = [(i, layer) for i in sorted(range(3), key=lambda i: (plan.wide[i], i)) for pair in range(half) for layer in (pair, half + pair)]

    def behind(rightward, steps):
        return lax.rem(me + n - steps if rightward else me + steps, n)

    def rows(i, device):
        return pl.ds(pl.multiple_of(device * plan.block[i], ROWS), plan.block[i])

    def send(rightward, source, target, send_sem, recv_sem):
        return pltpu.make_async_remote_copy(
            src_ref=source,
            dst_ref=target,
            send_sem=send_sem,
            recv_sem=recv_sem,
            device_id={AXIS: right if rightward else left},
            device_id_type=MESH,
        )

    def first_copy(i, layer):
        rightward = layer < half
        source = terms[i].at[0, layer, rows(i, behind(rightward, 1))]
        return send(rightward, source, first[i].at[layer], first_send.at[i, layer], first_recv.at[i, layer])

    def sum_copy(at, step):
        rightward, tile, count, _ = plan.sums[at]
        part = pl.ds(tile, count)
        return send(rightward, sums.at[step - 1, part], sums.at[step, part], sum_send.at[step - 1, at], sum_recv.at[step - 1, at])

    def out_copy(at, step):
        rightward, tile, count, _ = plan.news[at]
        piece = news.at[behind(rightward, step), pl.ds(tile, count)]
        return send(rightward, piece, piece, out_send.at[step, at], out_recv.at[step, at])

    def load(i, layer, steps):
        part = rows(i, behind(layer < half, steps))
        return pltpu.make_async_copy(terms[i].at[0, layer, part], held[i].at[layer, part], held_sem.at[i, layer, steps - 2])

    def own_load(i):
        return pltpu.make_async_copy(weights[i].at[:, rows(i, me)], own[i], own_sem.at[i])

    def moment_load(i):
        return (pltpu.make_async_copy(ms[i], new_m[i], m_sem.at[i]), pltpu.make_async_copy(vs[i], new_v[i], v_sem.at[i]))

    def each_tile(runs, body):
        for layer, i, row, count, tile in runs:

            @pl.loop(0, count)
            def _(k, layer=layer, i=i, row=row, tile=tile):
                for column in range(plan.wide[i]):
                    body(layer, i, (row + k) * ROWS, column * LANES, tile + k * plan.wide[i] + column)

    def tile_of(ref, layer, row, column):
        return ref[layer, pl.ds(pl.multiple_of(row, ROWS), ROWS), pl.ds(column, LANES)]

    def term(i, layer, steps, row, column):
        device = behind(layer < half, steps)
        return tile_of(held[i], layer, device * plan.block[i] + row, column).astype(jnp.float32)

    barrier = pltpu.get_barrier_semaphore()

    @pl.when(me < n - 1)
    def _():
        pl.semaphore_signal(barrier, inc=1, device_id={AXIS: right}, device_id_type=MESH)

    @pl.when(me == 0)
    def _():
        pl.semaphore_signal(barrier, inc=1, device_id={AXIS: left}, device_id_type=MESH)

    def start(rightward):
        for i, layer in every:
            if (layer < half) == rightward:
                first_copy(i, layer).start()


    @pl.when(me > 0)
    def _():
        pl.semaphore_wait(barrier, 1 + (me == n - 1).astype(jnp.int32))
        pl.semaphore_signal(entered.at[1], inc=1, device_id={AXIS: left}, device_id_type=MESH)

    @pl.when(me == n - 1)
    def _():
        pl.semaphore_signal(entered.at[0], inc=1, device_id={AXIS: right}, device_id_type=MESH)
        start(True)

    @pl.when(me > 0)
    def _():
        start(False)

    @pl.when(me < n - 1)
    def _():
        pl.semaphore_wait(entered.at[1], 1)
        start(True)

    @pl.when(me == 0)
    def _():
        pl.semaphore_wait(entered.at[0], 1)
        start(False)

    for steps in range(2, n + 1):
        for i, layer in every:
            load(i, layer, steps).start()
    for i in range(3):
        own_load(i).start()
        for copy in moment_load(i):
            copy.start()

    def wait_loads(runs, steps):
        for layer, i, row, _, _ in runs:
            if row == 0:
                load(i, layer, steps).wait()

    arrived = set()
    for at, (rightward, _, _, runs) in enumerate(plan.sums):
        for layer, i, row, _, _ in runs:
            if (i, layer) not in arrived:
                first_copy(i, layer).wait_recv()
                arrived.add((i, layer))
        wait_loads(runs, 2)

        def add_first(layer, i, row, column, tile):
            sums[0, tile] = (tile_of(first[i], layer, row, column).astype(jnp.float32) + term(i, layer, 2, row, column)).astype(jnp.bfloat16)

        each_tile(runs, add_first)
        sum_copy(at, 1).start()

    @pl.loop(1, n - 2)
    def _(step):
        for at, (rightward, _, _, runs) in enumerate(plan.sums):
            sum_copy(at, step).wait_recv()
            wait_loads(runs, step + 2)

            def add(layer, i, row, column, tile):
                sums[step, tile] = (sums[step, tile].astype(jnp.float32) + term(i, layer, step + 2, row, column)).astype(jnp.bfloat16)

            each_tile(runs, add)
            sum_copy(at, step + 1).start()

    for i in range(3):
        own_load(i).wait()
        for copy in moment_load(i):
            copy.wait()

    for at, (rightward, _, _, runs) in enumerate(plan.sums):
        sum_copy(at, n - 2).wait_recv()
        wait_loads(runs, n)

        def take_step(layer, i, row, column, tile):
            g = (sums[n - 2, tile].astype(jnp.float32) + term(i, layer, n, row, column)).astype(jnp.bfloat16).astype(jnp.float32)
            place = (layer, pl.ds(pl.multiple_of(row, ROWS), ROWS), pl.ds(column, LANES))
            w, m, v = adamw(own[i][place].astype(jnp.float32), new_m[i][place], new_v[i][place], g)
            news[me, tile] = w
            new_w[i][layer, pl.ds(pl.multiple_of(me * plan.block[i] + row, ROWS), ROWS), pl.ds(column, LANES)] = w
            new_m[i][place] = m
            new_v[i][place] = v

        each_tile(runs, take_step)
        out_copy(at, 0).start()

    for i, layer in every:
        first_copy(i, layer).wait_send()

    def deal(at, step):
        rightward, _, _, runs = plan.news[at]
        device = behind(rightward, step + 1)

        def move(layer, i, row, column, tile):
            new_w[i][layer, pl.ds(pl.multiple_of(device * plan.block[i] + row, ROWS), ROWS), pl.ds(column, LANES)] = news[device, tile]

        each_tile(runs, move)

    @pl.loop(0, n - 2)
    def _(step):
        for at in range(len(plan.news)):
            out_copy(at, step).wait_recv()
            out_copy(at, step + 1).start()
            deal(at, step)
        for at in range(len(plan.news)):
            sum_copy(at, step + 1).wait_send()

        @pl.when(step > 0)
        def _():
            for at in range(len(plan.news)):
                out_copy(at, step - 1).wait_send()

    for at in range(len(plan.news)):
        out_copy(at, n - 3).wait_send()
    for at in range(len(plan.news)):
        out_copy(at, n - 2).wait_recv()
        deal(at, n - 2)
    for at in range(len(plan.news)):
        out_copy(at, n - 2).wait_send()


def put(*refs):
    count = len(refs) // 2
    copies = [pltpu.make_async_copy(refs[i], refs[count + i], refs[-1].at[i]) for i in range(count)]
    for copy in copies:
        copy.start()
    for copy in copies:
        copy.wait()


def solution(mesh):
    n = mesh.shape[AXIS]

    def step(*arrays):
        terms, weights, m, v = (arrays[i : i + 3] for i in (0, 3, 6, 9))
        plan = Plan([one.shape for one in m])
        layers = plan.layers
        dma, kind = pltpu.SemaphoreType.DMA, weights[0].dtype
        arrays = [pltpu.with_memory_space_constraint(one, pltpu.HBM) for one in arrays]
        new = pl.pallas_call(
            functools.partial(kernel, n, plan),
            out_shape=tuple(pltpu.VMEM(one.shape, one.dtype) for one in weights + m + v),
            in_specs=[pl.BlockSpec(memory_space=pltpu.HBM)] * 12,
            out_specs=(pl.BlockSpec(memory_space=pltpu.VMEM),) * 9,
            scratch_shapes=[pltpu.VMEM(w.shape, kind) for w in weights]
            + [pltpu.VMEM(one.shape, kind) for one in m + m]
            + [pltpu.VMEM((n - 1, plan.tiles, ROWS, LANES), kind), pltpu.VMEM((n, plan.tiles, ROWS, LANES), kind)]
            + [pltpu.SemaphoreType.REGULAR((2,)), dma((3, layers, n - 1)), dma((3,)), dma((3,)), dma((3,))]
            + [dma((3, layers))] * 2
            + [dma((n - 2, len(plan.sums)))] * 2
            + [dma((n - 1, len(plan.news)))] * 2,
            compiler_params=pltpu.CompilerParams(collective_id=0, has_side_effects=True, vmem_limit_bytes=40 * 2**20),
        )(*arrays)
        new = [pltpu.with_memory_space_constraint(one, pltpu.VMEM) for one in new]
        return pl.pallas_call(
            put,
            out_shape=tuple(pltpu.HBM(one.shape, one.dtype) for one in weights + m + v),
            in_specs=[pl.BlockSpec(memory_space=pltpu.VMEM)] * 9,
            out_specs=(pl.BlockSpec(memory_space=pltpu.HBM),) * 9,
            scratch_shapes=[dma((9,))],
            compiler_params=pltpu.CompilerParams(vmem_limit_bytes=2**20),
        )(*new)

    all_of, part = P(None, None, None), P(None, AXIS, None)
    return jax.shard_map(
        step,
        mesh=mesh,
        in_specs=(P(("rep", AXIS), None, None, None),) * 3 + (all_of,) * 3 + (part,) * 6,
        out_specs=(P("rep", None, None),) * 3 + (P("rep", AXIS, None),) * 6,
        check_vma=False,
    )
```

time: 275 us -> 164 us (0.60)
  waiting for transfers between devices: 245 us -> 0 us
  Pallas kernels: 0 us -> 164 us
  between operations: 14.2 us -> 0.65 us
  local copies, waits for them, and re-layouts: 7.76 us -> 0 us
  other arithmetic: 7.18 us -> 0 us
    pallas_call x0 -> x2, Pallas kernels: none -> 164 us  [the longest x1 159 us: step(): pl.pallas_call(functools.partial(kernel, n, plan), out_shape=tuple((pltpu...]
    reduce_scatter x3 -> x0, waiting for transfers between devices: 126 us -> none  [step(): lax.psum_scatter(t[0], 'dp', scatter_dimension=1, tiled=True)]
    all_gather x3 -> x0, waiting for transfers between devices: 117 us -> none  [step(): whole = [lax.all_gather(one[0], 'dp', axis=1, tiled=True) for one in new]]
    unnamed x19 -> x0, local copies, waits for them, and re-layouts: 7.76 us -> none
    convert_element_type x3 -> x0, other arithmetic: 7.18 us -> none  [adamw(): return ((w - 0.02 * step).astype(jnp.bfloat16), m, v)]
  transfers between devices with their start and end apart: 6 -> 0, of which waited for: 6 -> 0; matrix products, arithmetic and copies ran while one was open for 3% -> 0% of each run, Pallas kernels for 0% -> 0%
where the time goes in v7:
time: 164 us
  Pallas kernels  164 us (100%)
    pallas_call x1, Pallas kernels, step(): pl.pallas_call(functools.partial(kernel, n, plan), out_shape=tuple((pltpu...  159 us
    pallas_call x1, Pallas kernels, step(): pl.pallas_call(put, out_shape=tuple((pltpu.HBM(one.shape, one.dtype) for...  4.42 us

profile of v7, /device:TPU:22, one launch (start us, length us, event | category | flops | bytes accessed | tf_op | source)
XLA Modules:
  0.0 164.4 jit_solution(15382512913942932513)
XLA Ops:
  0.6 159.3 %shard_map.187 = (bf16[2,512,1280]{2,1,0:T(8,128)(2,1)S(1)}, bf16[2,512,1280]{2,1,0:T(8,128)(2,1)S(1)}, bf16[2,1280,512]{2,1,0:T(8,128)(2,1)S(1)}, f32[2,64,1280...) custom-call(bf16[1,2,512,1280]{3,2,1,0:T(8,128)(2,1)} %refs_0_.1, ...), custom_call_target="tpu_custom_call" | custom-call | tf_op jit(solution)/shard_map/pallas_call | solution.py:282
  160.0 4.4 %shard_map.188 = (bf16[2,512,1280]{2,1,0:T(8,128)(2,1)}, bf16[2,512,1280]{2,1,0:T(8,128)(2,1)}, bf16[2,1280,512]{2,1,0:T(8,128)(2,1)}, f32[2,64,1280]{2,1,0:T(8,...) custom-call(bf16[2,512,1280]{2,1,0:T(8,128)(2,1)S(1)} %get-tuple-ele, ...), custom_call_target="tpu_custom_call" | custom-call | tf_op jit(solution)/shard_map/pallas_call | solution.py:297

commit v8 on v7

--- a/solution.py
+++ b/solution.py
@@ -10,15 +10,13 @@
 AXIS = "dp"
 MESH = pl.DeviceIdType.MESH
 ROWS, LANES = 16, 128
-MOVED = 1
-
+SHORTER = 3
 
 def adamw(w, m, v, g):
     m = 0.9 * m + 0.1 * g
     v = 0.95 * v + 0.05 * g * g
     step = m * lax.rsqrt(v + 1e-8) + 0.1 * w
     return (w - 0.02 * step).astype(jnp.bfloat16), m, v
-
 
 class Plan:
     def __init__(self, shapes):
@@ -36,20 +34,17 @@
                         bands[rightward].append((layer, i, row, tile))
                         tile += self.wide[i]
         self.tiles = tile
-        self.sums = self.cut(bands[False], bands[True])
-        self.news = self.cut(bands[False] + bands[True][:MOVED], bands[True][MOVED:])
-
-    def cut(self, left, right):
-        copies = []
-        for rightward, bands in ((True, right), (False, left)):
-            count = sum(self.wide[i] for _, i, _, _ in bands)
-            at = next(k for k, band in enumerate(bands) if 2 * (band[3] - bands[0][3]) >= count - self.wide[band[1]])
-            copies.append([(rightward, part) for part in (bands[:at], bands[at:])])
-        return [
+        ways = []
+        for rightward in (True, False):
+            all_of, start = bands[rightward], bands[rightward][0][3]
+            at = next(k for k, band in enumerate(all_of) if 2 * (band[3] - start) >= self.tiles // 2)
+            ways.append([(rightward, part) for part in (all_of[:at], all_of[at:])])
+        self.copies = [
             (rightward, part[0][3], sum(self.wide[i] for _, i, _, _ in part), self.runs(part))
-            for pair in zip(*copies)
+            for pair in zip(*ways, strict=True)
             for rightward, part in pair
         ]
+        self.left_out = sum(self.wide[i] for _, i, _, _ in bands[True][-SHORTER:])
 
     def runs(self, bands):
         runs = []
@@ -60,11 +55,10 @@
                 runs.append([layer, i, row, 1, tile])
         return runs
 
-
 def kernel(n, plan, *refs):
     terms, weights, ms, vs = (refs[i : i + 3] for i in (0, 3, 6, 9))
     new_w, new_m, new_v, held, own, first = (refs[i : i + 3] for i in (12, 15, 18, 21, 24, 27))
-    sums, news, entered, held_sem, own_sem, m_sem, v_sem, first_send, first_recv, sum_send, sum_recv, out_send, out_recv = refs[30:]
+    sums, news, entered, held_sem, own_sem, m_sem, v_sem, first_send, first_recv, sum_send, sum_recv, out_send, out_recv, end_send, end_recv = refs[30:]
     me = lax.axis_index(AXIS)
     right, left = lax.rem(me + 1, n), lax.rem(me + n - 1, n)
     half = plan.layers // 2
@@ -92,14 +86,20 @@
         return send(rightward, source, first[i].at[layer], first_send.at[i, layer], first_recv.at[i, layer])
 
     def sum_copy(at, step):
-        rightward, tile, count, _ = plan.sums[at]
+        rightward, tile, count, _ = plan.copies[at]
         part = pl.ds(tile, count)
         return send(rightward, sums.at[step - 1, part], sums.at[step, part], sum_send.at[step - 1, at], sum_recv.at[step - 1, at])
 
-    def out_copy(at, step):
-        rightward, tile, count, _ = plan.news[at]
+    def out_copy(at, step, left_out=0):
+        rightward, tile, count, _ = plan.copies[at]
+        count -= left_out
         piece = news.at[behind(rightward, step), pl.ds(tile, count)]
         return send(rightward, piece, piece, out_send.at[step, at], out_recv.at[step, at])
+
+    def end_copy(at):
+        rightward, tile, count, _ = plan.copies[at]
+        piece = news.at[me, pl.ds(tile + count - plan.left_out, plan.left_out)]
+        return send(not rightward, piece, piece, end_send.at[int(rightward)], end_recv.at[int(rightward)])
 
     def load(i, layer, steps):
         part = rows(i, behind(layer < half, steps))
@@ -128,11 +128,11 @@
 
     barrier = pltpu.get_barrier_semaphore()
 
-    @pl.when(me < n - 1)
+    @pl.when(me < n - 2)
     def _():
         pl.semaphore_signal(barrier, inc=1, device_id={AXIS: right}, device_id_type=MESH)
 
-    @pl.when(me == 0)
+    @pl.when((me == 0) | (me == n - 1))
     def _():
         pl.semaphore_signal(barrier, inc=1, device_id={AXIS: left}, device_id_type=MESH)
 
@@ -141,27 +141,26 @@
             if (layer < half) == rightward:
                 first_copy(i, layer).start()
 
-
     @pl.when(me > 0)
     def _():
-        pl.semaphore_wait(barrier, 1 + (me == n - 1).astype(jnp.int32))
+        pl.semaphore_wait(barrier, 1 + (me == n - 2).astype(jnp.int32))
+
+    @pl.when((me > 0) & (me < n - 1))
+    def _():
         pl.semaphore_signal(entered.at[1], inc=1, device_id={AXIS: left}, device_id_type=MESH)
-
-    @pl.when(me == n - 1)
+        start(False)
+
+    @pl.when(me >= n - 2)
     def _():
         pl.semaphore_signal(entered.at[0], inc=1, device_id={AXIS: right}, device_id_type=MESH)
         start(True)
 
-    @pl.when(me > 0)
-    def _():
-        start(False)
-
-    @pl.when(me < n - 1)
+    @pl.when(me < n - 2)
     def _():
         pl.semaphore_wait(entered.at[1], 1)
         start(True)
 
-    @pl.when(me == 0)
+    @pl.when((me == 0) | (me == n - 1))
     def _():
         pl.semaphore_wait(entered.at[0], 1)
         start(False)
@@ -180,7 +179,7 @@
                 load(i, layer, steps).wait()
 
     arrived = set()
-    for at, (rightward, _, _, runs) in enumerate(plan.sums):
+    for at, (rightward, _, _, runs) in enumerate(plan.copies):
         for layer, i, row, _, _ in runs:
             if (i, layer) not in arrived:
                 first_copy(i, layer).wait_recv()
@@ -195,7 +194,7 @@
 
     @pl.loop(1, n - 2)
     def _(step):
-        for at, (rightward, _, _, runs) in enumerate(plan.sums):
+        for at, (rightward, _, _, runs) in enumerate(plan.copies):
             sum_copy(at, step).wait_recv()
             wait_loads(runs, step + 2)
 
@@ -210,7 +209,7 @@
         for copy in moment_load(i):
             copy.wait()
 
-    for at, (rightward, _, _, runs) in enumerate(plan.sums):
+    for at, (rightward, _, _, runs) in enumerate(plan.copies):
         sum_copy(at, n - 2).wait_recv()
         wait_loads(runs, n)
 
@@ -230,7 +229,7 @@
         first_copy(i, layer).wait_send()
 
     def deal(at, step):
-        rightward, _, _, runs = plan.news[at]
+        rightward, _, _, runs = plan.copies[at]
         device = behind(rightward, step + 1)
 
         def move(layer, i, row, column, tile):
@@ -238,28 +237,57 @@
 
         each_tile(runs, move)
 
-    @pl.loop(0, n - 2)
+    @pl.loop(0, n - 3)
     def _(step):
-        for at in range(len(plan.news)):
+        for at in range(len(plan.copies)):
             out_copy(at, step).wait_recv()
             out_copy(at, step + 1).start()
             deal(at, step)
-        for at in range(len(plan.news)):
+        for at in range(len(plan.copies)):
             sum_copy(at, step + 1).wait_send()
 
         @pl.when(step > 0)
         def _():
-            for at in range(len(plan.news)):
+            for at in range(len(plan.copies)):
                 out_copy(at, step - 1).wait_send()
 
-    for at in range(len(plan.news)):
+    ends = range(len(plan.copies) - 2, len(plan.copies))
+
+    def last(at, shorter, do):
+        if at not in ends:
+            do(out_copy(at, n - 2))
+            return
+        pl.when(shorter)(lambda: do(out_copy(at, n - 2, plan.left_out)))
+        pl.when(jnp.logical_not(shorter))(lambda: do(out_copy(at, n - 2)))
+
+    def sends_shorter(at):
+        return me == (n - 1 if plan.copies[at][0] else 0)
+
+    def gets_shorter(at):
+        return me == (0 if plan.copies[at][0] else n - 1)
+
+    def sends_end(at):
+        return me == (1 if plan.copies[at][0] else n - 2)
+
+    for at in range(len(plan.copies)):
+        out_copy(at, n - 3).wait_recv()
+        last(at, sends_shorter(at), lambda copy: copy.start())
+        if at in ends:
+            pl.when(sends_end(at))(lambda at=at: end_copy(at).start())
+        deal(at, n - 3)
+    for at in range(len(plan.copies)):
+        sum_copy(at, n - 2).wait_send()
+        out_copy(at, n - 4).wait_send()
         out_copy(at, n - 3).wait_send()
-    for at in range(len(plan.news)):
-        out_copy(at, n - 2).wait_recv()
+    for at in range(len(plan.copies)):
+        last(at, gets_shorter(at), lambda copy: copy.wait_recv())
+        if at in ends:
+            pl.when(gets_shorter(at))(lambda at=at: end_copy(at).wait_recv())
         deal(at, n - 2)
-    for at in range(len(plan.news)):
-        out_copy(at, n - 2).wait_send()
-
+    for at in range(len(plan.copies)):
+        last(at, sends_shorter(at), lambda copy: copy.wait_send())
+        if at in ends:
+            pl.when(sends_end(at))(lambda at=at: end_copy(at).wait_send())
 
 def put(*refs):
     count = len(refs) // 2
@@ -268,7 +296,6 @@
         copy.start()
     for copy in copies:
         copy.wait()
-
 
 def solution(mesh):
     n = mesh.shape[AXIS]
@@ -289,8 +316,9 @@
             + [pltpu.VMEM((n - 1, plan.tiles, ROWS, LANES), kind), pltpu.VMEM((n, plan.tiles, ROWS, LANES), kind)]
             + [pltpu.SemaphoreType.REGULAR((2,)), dma((3, layers, n - 1)), dma((3,)), dma((3,)), dma((3,))]
             + [dma((3, layers))] * 2
-            + [dma((n - 2, len(plan.sums)))] * 2
-            + [dma((n - 1, len(plan.news)))] * 2,
+            + [dma((n - 2, len(plan.copies)))] * 2
+            + [dma((n - 1, len(plan.copies)))] * 2
+            + [dma((2,))] * 2,
             compiler_params=pltpu.CompilerParams(collective_id=0, has_side_effects=True, vmem_limit_bytes=40 * 2**20),
         )(*arrays)
         new = [pltpu.with_memory_space_constraint(one, pltpu.VMEM) for one in new]

time: 164 us -> 160 us (0.976)
  Pallas kernels: 164 us -> 160 us
    pallas_call x1, Pallas kernels: 159 us -> 155 us  [step(): pl.pallas_call(functools.partial(kernel, n, plan), out_shape=tuple((pltpu...]
where the time goes in v8:
time: 160 us
  Pallas kernels  160 us (100%)
    pallas_call x1, Pallas kernels, step(): pl.pallas_call(functools.partial(kernel, n, plan), out_shape=tuple((pltpu...  155 us
    pallas_call x1, Pallas kernels, step(): pl.pallas_call(put, out_shape=tuple((pltpu.HBM(one.shape, one.dtype) for...  4.42 us

profile of v8, /device:TPU:22, one launch (start us, length us, event | category | flops | bytes accessed | tf_op | source)
XLA Modules:
  0.0 160.2 jit_solution(13859197103697803923)
XLA Ops:
  0.6 155.1 %shard_map.187 = (bf16[2,512,1280]{2,1,0:T(8,128)(2,1)S(1)}, bf16[2,512,1280]{2,1,0:T(8,128)(2,1)S(1)}, bf16[2,1280,512]{2,1,0:T(8,128)(2,1)S(1)}, f32[2,64,1280...) custom-call(bf16[1,2,512,1280]{3,2,1,0:T(8,128)(2,1)} %refs_0_.1, ...), custom_call_target="tpu_custom_call" | custom-call | tf_op jit(solution)/shard_map/pallas_call | solution.py:309
  155.8 4.4 %shard_map.188 = (bf16[2,512,1280]{2,1,0:T(8,128)(2,1)}, bf16[2,512,1280]{2,1,0:T(8,128)(2,1)}, bf16[2,1280,512]{2,1,0:T(8,128)(2,1)}, f32[2,64,1280]{2,1,0:T(8,...) custom-call(bf16[2,512,1280]{2,1,0:T(8,128)(2,1)S(1)} %get-tuple-ele, ...), custom_call_target="tpu_custom_call" | custom-call | tf_op jit(solution)/shard_map/pallas_call | solution.py:325

commit v9 on v8

--- a/solution.py
+++ b/solution.py
@@ -10,7 +10,7 @@
 AXIS = "dp"
 MESH = pl.DeviceIdType.MESH
 ROWS, LANES = 16, 128
-SHORTER = 3
+SHORTER = 4
 
 def adamw(w, m, v, g):
     m = 0.9 * m + 0.1 * g
@@ -111,10 +111,10 @@
     def moment_load(i):
         return (pltpu.make_async_copy(ms[i], new_m[i], m_sem.at[i]), pltpu.make_async_copy(vs[i], new_v[i], v_sem.at[i]))
 
-    def each_tile(runs, body):
+    def each_tile(runs, body, unroll=False):
         for layer, i, row, count, tile in runs:
 
-            @pl.loop(0, count)
+            @pl.loop(0, count, unroll=unroll)
             def _(k, layer=layer, i=i, row=row, tile=tile):
                 for column in range(plan.wide[i]):
                     body(layer, i, (row + k) * ROWS, column * LANES, tile + k * plan.wide[i] + column)
@@ -228,14 +228,14 @@
     for i, layer in every:
         first_copy(i, layer).wait_send()
 
-    def deal(at, step):
+    def deal(at, step, unroll=False):
         rightward, _, _, runs = plan.copies[at]
         device = behind(rightward, step + 1)
 
         def move(layer, i, row, column, tile):
             new_w[i][layer, pl.ds(pl.multiple_of(device * plan.block[i] + row, ROWS), ROWS), pl.ds(column, LANES)] = news[device, tile]
 
-        each_tile(runs, move)
+        each_tile(runs, move, unroll)
 
     @pl.loop(0, n - 3)
     def _(step):
@@ -283,7 +283,7 @@
         last(at, gets_shorter(at), lambda copy: copy.wait_recv())
         if at in ends:
             pl.when(gets_shorter(at))(lambda at=at: end_copy(at).wait_recv())
-        deal(at, n - 2)
+        deal(at, n - 2, True)
     for at in range(len(plan.copies)):
         last(at, sends_shorter(at), lambda copy: copy.wait_send())
         if at in ends:

time: 160 us -> 161 us (level)
  no operation moved by 1% of the time
where the time goes in v9:
time: 161 us
  Pallas kernels  160 us (99%)
    pallas_call x1, Pallas kernels, step(): pl.pallas_call(functools.partial(kernel, n, plan), out_shape=tuple((pltpu...  156 us
    pallas_call x1, Pallas kernels, step(): pl.pallas_call(put, out_shape=tuple((pltpu.HBM(one.shape, one.dtype) for...  4.42 us

profile of v9, /device:TPU:22, one launch (start us, length us, event | category | flops | bytes accessed | tf_op | source)
XLA Modules:
  0.0 161.1 jit_solution(17352218611412488174)
XLA Ops:
  0.6 156.0 %shard_map.187 = (bf16[2,512,1280]{2,1,0:T(8,128)(2,1)S(1)}, bf16[2,512,1280]{2,1,0:T(8,128)(2,1)S(1)}, bf16[2,1280,512]{2,1,0:T(8,128)(2,1)S(1)}, f32[2,64,1280...) custom-call(bf16[1,2,512,1280]{3,2,1,0:T(8,128)(2,1)} %refs_0_.1, ...), custom_call_target="tpu_custom_call" | custom-call | tf_op jit(solution)/shard_map/pallas_call | solution.py:309
  156.7 4.4 %shard_map.188 = (bf16[2,512,1280]{2,1,0:T(8,128)(2,1)}, bf16[2,512,1280]{2,1,0:T(8,128)(2,1)}, bf16[2,1280,512]{2,1,0:T(8,128)(2,1)}, f32[2,64,1280]{2,1,0:T(8,...) custom-call(bf16[2,512,1280]{2,1,0:T(8,128)(2,1)S(1)} %get-tuple-ele, ...), custom_call_target="tpu_custom_call" | custom-call | tf_op jit(solution)/shard_map/pallas_call | solution.py:325

commit v10 on v9

--- a/solution.py
+++ b/solution.py
@@ -10,7 +10,8 @@
 AXIS = "dp"
 MESH = pl.DeviceIdType.MESH
 ROWS, LANES = 16, 128
-SHORTER = 4
+LEFT_OUT = {True: 38, False: 16}
+AROUND = 80
 
 def adamw(w, m, v, g):
     m = 0.9 * m + 0.1 * g
@@ -24,12 +25,12 @@
         self.block = [shape[1] for shape in shapes]
         self.wide = [shape[2] // LANES for shape in shapes]
         half = self.layers // 2
-        order = sorted(range(len(shapes)), key=lambda i: (self.wide[i], i))
+        self.order = sorted(range(len(shapes)), key=lambda i: (self.wide[i], i))
         bands, tile = {}, 0
         for rightward in (False, True):
             bands[rightward] = []
             for layer in range(half) if rightward else range(half, self.layers):
-                for i in order:
+                for i in self.order:
                     for row in range(self.block[i] // ROWS):
                         bands[rightward].append((layer, i, row, tile))
                         tile += self.wide[i]
@@ -44,7 +45,6 @@
             for pair in zip(*ways, strict=True)
             for rightward, part in pair
         ]
-        self.left_out = sum(self.wide[i] for _, i, _, _ in bands[True][-SHORTER:])
 
     def runs(self, bands):
         runs = []
@@ -58,11 +58,12 @@
 def kernel(n, plan, *refs):
     terms, weights, ms, vs = (refs[i : i + 3] for i in (0, 3, 6, 9))
     new_w, new_m, new_v, held, own, first = (refs[i : i + 3] for i in (12, 15, 18, 21, 24, 27))
-    sums, news, entered, held_sem, own_sem, m_sem, v_sem, first_send, first_recv, sum_send, sum_recv, out_send, out_recv, end_send, end_recv = refs[30:]
+    around, around_send, around_recv = refs[-3:]
+    sums, news, entered, held_sem, own_sem, m_sem, v_sem, first_send, first_recv, sum_send, sum_recv, out_send, out_recv, end_send, end_recv = refs[30:-3]
     me = lax.axis_index(AXIS)
     right, left = lax.rem(me + 1, n), lax.rem(me + n - 1, n)
     half = plan.layers // 2
-    every = [(i, layer) for i in sorted(range(3), key=lambda i: (plan.wide[i], i)) for pair in range(half) for layer in (pair, half + pair)]
+    every = [(i, layer) for i in plan.order for pair in range(half) for layer in (pair, half + pair)]
 
     def behind(rightward, steps):
         return lax.rem(me + n - steps if rightward else me + steps, n)
@@ -80,10 +81,28 @@
             device_id_type=MESH,
         )
 
-    def first_copy(i, layer):
-        rightward = layer < half
-        source = terms[i].at[0, layer, rows(i, behind(rightward, 1))]
-        return send(rightward, source, first[i].at[layer], first_send.at[i, layer], first_recv.at[i, layer])
+    def first_copy(i, layer, skip=0):
+        rightward, count = layer < half, plan.block[i] - skip
+        source = terms[i].at[0, layer, pl.ds(pl.multiple_of(behind(rightward, 1) * plan.block[i] + skip, ROWS), count)]
+        return send(rightward, source, first[i].at[layer, pl.ds(skip, count)], first_send.at[i, layer], first_recv.at[i, layer])
+
+    split = plan.order[0], half
+    splits, gets_rest, gets_around = me <= 1, (me == 0) | (me == n - 1), (me == 1) | (me == 2)
+
+    def around_copy():
+        i, layer = split
+        source = terms[i].at[0, layer, pl.ds(pl.multiple_of(behind(False, 1) * plan.block[i], ROWS), AROUND)]
+        return send(True, source, around, around_send, around_recv)
+
+    def either(shorter, short, full, do):
+        pl.when(shorter)(lambda: do(short()))
+        pl.when(jnp.logical_not(shorter))(lambda: do(full()))
+
+    def first_of(i, layer, shorter, do):
+        if (i, layer) == split:
+            either(shorter, lambda: first_copy(i, layer, AROUND), lambda: first_copy(i, layer), do)
+        else:
+            do(first_copy(i, layer))
 
     def sum_copy(at, step):
         rightward, tile, count, _ = plan.copies[at]
@@ -98,7 +117,7 @@
 
     def end_copy(at):
         rightward, tile, count, _ = plan.copies[at]
-        piece = news.at[me, pl.ds(tile + count - plan.left_out, plan.left_out)]
+        piece = news.at[me, pl.ds(tile + count - LEFT_OUT[rightward], LEFT_OUT[rightward])]
         return send(not rightward, piece, piece, end_send.at[int(rightward)], end_recv.at[int(rightward)])
 
     def load(i, layer, steps):
@@ -139,7 +158,7 @@
     def start(rightward):
         for i, layer in every:
             if (layer < half) == rightward:
-                first_copy(i, layer).start()
+                first_of(i, layer, splits, lambda copy: copy.start())
 
     @pl.when(me > 0)
     def _():
@@ -160,10 +179,23 @@
         pl.semaphore_wait(entered.at[1], 1)
         start(True)
 
+    @pl.when(splits)
+    def _():
+        around_copy().start()
+
     @pl.when((me == 0) | (me == n - 1))
     def _():
         pl.semaphore_wait(entered.at[0], 1)
         start(False)
+
+    @pl.when(gets_rest)
+    def _():
+        i, layer = split
+        first[i][layer, pl.ds(0, AROUND)] = jnp.zeros((AROUND, first[i].shape[2]), first[i].dtype)
+
+    @pl.when(jnp.logical_not(gets_around))
+    def _():
+        around[...] = jnp.zeros_like(around)
 
     for steps in range(2, n + 1):
         for i, layer in every:
@@ -182,7 +214,7 @@
     for at, (rightward, _, _, runs) in enumerate(plan.copies):
         for layer, i, row, _, _ in runs:
             if (i, layer) not in arrived:
-                first_copy(i, layer).wait_recv()
+                first_of(i, layer, gets_rest, lambda copy: copy.wait_recv())
                 arrived.add((i, layer))
         wait_loads(runs, 2)
 
@@ -213,8 +245,11 @@
         sum_copy(at, n - 2).wait_recv()
         wait_loads(runs, n)
 
-        def take_step(layer, i, row, column, tile):
-            g = (sums[n - 2, tile].astype(jnp.float32) + term(i, layer, n, row, column)).astype(jnp.bfloat16).astype(jnp.float32)
+        def take_step(layer, i, row, column, tile, more=None):
+            g = sums[n - 2, tile].astype(jnp.float32) + term(i, layer, n, row, column)
+            if more is not None:
+                g += more[pl.ds(pl.multiple_of(row, ROWS), ROWS), pl.ds(column, LANES)].astype(jnp.float32)
+            g = g.astype(jnp.bfloat16).astype(jnp.float32)
             place = (layer, pl.ds(pl.multiple_of(row, ROWS), ROWS), pl.ds(column, LANES))
             w, m, v = adamw(own[i][place].astype(jnp.float32), new_m[i][place], new_v[i][place], g)
             news[me, tile] = w
@@ -222,11 +257,19 @@
             new_m[i][place] = m
             new_v[i][place] = v
 
-        each_tile(runs, take_step)
+        for run in runs:
+            layer, i, row, count, tile = run
+            if (i, layer) == split and row == 0:
+                pl.when(gets_around)(lambda: around_copy().wait_recv())
+                part = AROUND // ROWS
+                each_tile([(layer, i, row, part, tile)], functools.partial(take_step, more=around))
+                run = (layer, i, row + part, count - part, tile + part * plan.wide[i])
+            each_tile([run], take_step)
         out_copy(at, 0).start()
 
     for i, layer in every:
-        first_copy(i, layer).wait_send()
+        first_of(i, layer, splits, lambda copy: copy.wait_send())
+    pl.when(splits)(lambda: around_copy().wait_send())
 
     def deal(at, step, unroll=False):
         rightward, _, _, runs = plan.copies[at]
@@ -257,8 +300,8 @@
         if at not in ends:
             do(out_copy(at, n - 2))
             return
-        pl.when(shorter)(lambda: do(out_copy(at, n - 2, plan.left_out)))
-        pl.when(jnp.logical_not(shorter))(lambda: do(out_copy(at, n - 2)))
+        left_out = LEFT_OUT[plan.copies[at][0]]
+        either(shorter, lambda: out_copy(at, n - 2, left_out), lambda: out_copy(at, n - 2), do)
 
     def sends_shorter(at):
         return me == (n - 1 if plan.copies[at][0] else 0)
@@ -318,7 +361,8 @@
             + [dma((3, layers))] * 2
             + [dma((n - 2, len(plan.copies)))] * 2
             + [dma((n - 1, len(plan.copies)))] * 2
-            + [dma((2,))] * 2,
+            + [dma((2,))] * 2
+            + [pltpu.VMEM((AROUND, m[plan.order[0]].shape[2]), kind), dma, dma],
             compiler_params=pltpu.CompilerParams(collective_id=0, has_side_effects=True, vmem_limit_bytes=40 * 2**20),
         )(*arrays)
         new = [pltpu.with_memory_space_constraint(one, pltpu.VMEM) for one in new]

time: 161 us -> 161 us (level)
  no operation moved by 1% of the time
where the time goes in v10:
time: 161 us
  Pallas kernels  160 us (99%)
    pallas_call x1, Pallas kernels, step(): pl.pallas_call(functools.partial(kernel, n, plan), out_shape=tuple((pltpu...  156 us
    pallas_call x1, Pallas kernels, step(): pl.pallas_call(put, out_shape=tuple((pltpu.HBM(one.shape, one.dtype) for...  4.42 us

profile of v10, /device:TPU:22, one launch (start us, length us, event | category | flops | bytes accessed | tf_op | source)
XLA Modules:
  0.0 160.9 jit_solution(12149141437629319569)
XLA Ops:
  0.6 155.8 %shard_map.187 = (bf16[2,512,1280]{2,1,0:T(8,128)(2,1)S(1)}, bf16[2,512,1280]{2,1,0:T(8,128)(2,1)S(1)}, bf16[2,1280,512]{2,1,0:T(8,128)(2,1)S(1)}, f32[2,64,1280...) custom-call(bf16[1,2,512,1280]{3,2,1,0:T(8,128)(2,1)} %refs_0_.1, ...), custom_call_target="tpu_custom_call" | custom-call | tf_op jit(solution)/shard_map/pallas_call | solution.py:352
  156.5 4.4 %shard_map.188 = (bf16[2,512,1280]{2,1,0:T(8,128)(2,1)}, bf16[2,512,1280]{2,1,0:T(8,128)(2,1)}, bf16[2,1280,512]{2,1,0:T(8,128)(2,1)}, f32[2,64,1280]{2,1,0:T(8,...) custom-call(bf16[2,512,1280]{2,1,0:T(8,128)(2,1)S(1)} %get-tuple-ele, ...), custom_call_target="tpu_custom_call" | custom-call | tf_op jit(solution)/shard_map/pallas_call | solution.py:369

commit v11 on v10

--- a/solution.py
+++ b/solution.py
@@ -36,7 +36,7 @@
                         tile += self.wide[i]
         self.tiles = tile
         ways = []
-        for rightward in (True, False):
+        for rightward in (False, True):
             all_of, start = bands[rightward], bands[rightward][0][3]
             at = next(k for k, band in enumerate(all_of) if 2 * (band[3] - start) >= self.tiles // 2)
             ways.append([(rightward, part) for part in (all_of[:at], all_of[at:])])

time: 161 us -> 160 us (level)
  no operation moved by 1% of the time
where the time goes in v11:
time: 160 us; the launch traced here: 159 us
  Pallas kernels  159 us (99%)
    pallas_call x1, Pallas kernels, step(): pl.pallas_call(functools.partial(kernel, n, plan), out_shape=tuple((pltpu...  154 us
    pallas_call x1, Pallas kernels, step(): pl.pallas_call(put, out_shape=tuple((pltpu.HBM(one.shape, one.dtype) for...  4.42 us

profile of v11, /device:TPU:22, one launch (start us, length us, event | category | flops | bytes accessed | tf_op | source)
XLA Modules:
  0.0 159.4 jit_solution(9450997451623407251)
XLA Ops:
  0.6 154.4 %shard_map.187 = (bf16[2,512,1280]{2,1,0:T(8,128)(2,1)S(1)}, bf16[2,512,1280]{2,1,0:T(8,128)(2,1)S(1)}, bf16[2,1280,512]{2,1,0:T(8,128)(2,1)S(1)}, f32[2,64,1280...) custom-call(bf16[1,2,512,1280]{3,2,1,0:T(8,128)(2,1)} %refs_0_.1, ...), custom_call_target="tpu_custom_call" | custom-call | tf_op jit(solution)/shard_map/pallas_call | solution.py:352
  155.0 4.4 %shard_map.188 = (bf16[2,512,1280]{2,1,0:T(8,128)(2,1)}, bf16[2,512,1280]{2,1,0:T(8,128)(2,1)}, bf16[2,1280,512]{2,1,0:T(8,128)(2,1)}, f32[2,64,1280]{2,1,0:T(8,...) custom-call(bf16[2,512,1280]{2,1,0:T(8,128)(2,1)S(1)} %get-tuple-ele, ...), custom_call_target="tpu_custom_call" | custom-call | tf_op jit(solution)/shard_map/pallas_call | solution.py:369

commit v12 on v11

--- a/solution.py
+++ b/solution.py
@@ -10,8 +10,8 @@
 AXIS = "dp"
 MESH = pl.DeviceIdType.MESH
 ROWS, LANES = 16, 128
-LEFT_OUT = {True: 38, False: 16}
-AROUND = 80
+LEFT_OUT = {True: 33, False: 16}
+AROUND = {True: 48, False: 80}
 
 def adamw(w, m, v, g):
     m = 0.9 * m + 0.1 * g
@@ -58,8 +58,8 @@
 def kernel(n, plan, *refs):
     terms, weights, ms, vs = (refs[i : i + 3] for i in (0, 3, 6, 9))
     new_w, new_m, new_v, held, own, first = (refs[i : i + 3] for i in (12, 15, 18, 21, 24, 27))
-    around, around_send, around_recv = refs[-3:]
-    sums, news, entered, held_sem, own_sem, m_sem, v_sem, first_send, first_recv, sum_send, sum_recv, out_send, out_recv, end_send, end_recv = refs[30:-3]
+    around, (around_send, around_recv) = {True: refs[-4], False: refs[-3]}, refs[-2:]
+    sums, news, entered, held_sem, own_sem, m_sem, v_sem, first_send, first_recv, sum_send, sum_recv, out_send, out_recv, end_send, end_recv = refs[30:-4]
     me = lax.axis_index(AXIS)
     right, left = lax.rem(me + 1, n), lax.rem(me + n - 1, n)
     half = plan.layers // 2
@@ -86,21 +86,25 @@
         source = terms[i].at[0, layer, pl.ds(pl.multiple_of(behind(rightward, 1) * plan.block[i] + skip, ROWS), count)]
         return send(rightward, source, first[i].at[layer, pl.ds(skip, count)], first_send.at[i, layer], first_recv.at[i, layer])
 
-    split = plan.order[0], half
-    splits, gets_rest, gets_around = me <= 1, (me == 0) | (me == n - 1), (me == 1) | (me == 2)
-
-    def around_copy():
-        i, layer = split
-        source = terms[i].at[0, layer, pl.ds(pl.multiple_of(behind(False, 1) * plan.block[i], ROWS), AROUND)]
-        return send(True, source, around, around_send, around_recv)
+    split = {(plan.order[0], 0): True, (plan.order[0], half): False}
+    splits = {True: me == n - 1, False: me <= 1}
+    gets_rest = {True: me == 0, False: (me == 0) | (me == n - 1)}
+    gets_around = {True: me == n - 2, False: (me == 1) | (me == 2)}
+
+    def around_copy(rightward):
+        i = plan.order[0]
+        part = pl.ds(pl.multiple_of(behind(rightward, 1) * plan.block[i], ROWS), AROUND[rightward])
+        source = terms[i].at[0, 0 if rightward else half, part]
+        return send(not rightward, source, around[rightward], around_send.at[int(rightward)], around_recv.at[int(rightward)])
 
     def either(shorter, short, full, do):
         pl.when(shorter)(lambda: do(short()))
         pl.when(jnp.logical_not(shorter))(lambda: do(full()))
 
     def first_of(i, layer, shorter, do):
-        if (i, layer) == split:
-            either(shorter, lambda: first_copy(i, layer, AROUND), lambda: first_copy(i, layer), do)
+        if (i, layer) in split:
+            rightward = split[i, layer]
+            either(shorter[rightward], lambda: first_copy(i, layer, AROUND[rightward]), lambda: first_copy(i, layer), do)
         else:
             do(first_copy(i, layer))
 
@@ -179,23 +183,25 @@
         pl.semaphore_wait(entered.at[1], 1)
         start(True)
 
-    @pl.when(splits)
-    def _():
-        around_copy().start()
 
     @pl.when((me == 0) | (me == n - 1))
     def _():
         pl.semaphore_wait(entered.at[0], 1)
         start(False)
 
-    @pl.when(gets_rest)
-    def _():
-        i, layer = split
-        first[i][layer, pl.ds(0, AROUND)] = jnp.zeros((AROUND, first[i].shape[2]), first[i].dtype)
-
-    @pl.when(jnp.logical_not(gets_around))
-    def _():
-        around[...] = jnp.zeros_like(around)
+    for (i, layer), rightward in split.items():
+
+        @pl.when(splits[rightward])
+        def _(rightward=rightward):
+            around_copy(rightward).start()
+
+        @pl.when(gets_rest[rightward])
+        def _(i=i, layer=layer, rightward=rightward):
+            first[i][layer, pl.ds(0, AROUND[rightward])] = jnp.zeros(around[rightward].shape, first[i].dtype)
+
+        @pl.when(jnp.logical_not(gets_around[rightward]))
+        def _(rightward=rightward):
+            around[rightward][...] = jnp.zeros_like(around[rightward])
 
     for steps in range(2, n + 1):
         for i, layer in every:
@@ -259,17 +265,18 @@
 
         for run in runs:
             layer, i, row, count, tile = run
-            if (i, layer) == split and row == 0:
-                pl.when(gets_around)(lambda: around_copy().wait_recv())
-                part = AROUND // ROWS
-                each_tile([(layer, i, row, part, tile)], functools.partial(take_step, more=around))
+            if (i, layer) in split and row == 0:
+                pl.when(gets_around[rightward])(lambda rightward=rightward: around_copy(rightward).wait_recv())
+                part = AROUND[rightward] // ROWS
+                each_tile([(layer, i, row, part, tile)], functools.partial(take_step, more=around[rightward]))
                 run = (layer, i, row + part, count - part, tile + part * plan.wide[i])
             each_tile([run], take_step)
         out_copy(at, 0).start()
 
     for i, layer in every:
         first_of(i, layer, splits, lambda copy: copy.wait_send())
-    pl.when(splits)(lambda: around_copy().wait_send())
+    for way in (True, False):
+        pl.when(splits[way])(lambda way=way: around_copy(way).wait_send())
 
     def deal(at, step, unroll=False):
         rightward, _, _, runs = plan.copies[at]
@@ -362,7 +369,8 @@
             + [dma((n - 2, len(plan.copies)))] * 2
             + [dma((n - 1, len(plan.copies)))] * 2
             + [dma((2,))] * 2
-            + [pltpu.VMEM((AROUND, m[plan.order[0]].shape[2]), kind), dma, dma],
+            + [pltpu.VMEM((AROUND[way], m[plan.order[0]].shape[2]), kind) for way in (True, False)]
+            + [dma((2,))] * 2,
             compiler_params=pltpu.CompilerParams(collective_id=0, has_side_effects=True, vmem_limit_bytes=40 * 2**20),
         )(*arrays)
         new = [pltpu.with_memory_space_constraint(one, pltpu.VMEM) for one in new]

time: 160 us -> 159 us (level)
  no operation moved by 1% of the time
where the time goes in v12:
time: 159 us
  Pallas kernels  158 us (99%)
    pallas_call x1, Pallas kernels, step(): pl.pallas_call(functools.partial(kernel, n, plan), out_shape=tuple((pltpu...  154 us
    pallas_call x1, Pallas kernels, step(): pl.pallas_call(put, out_shape=tuple((pltpu.HBM(one.shape, one.dtype) for...  4.42 us

profile of v12, /device:TPU:22, one launch (start us, length us, event | category | flops | bytes accessed | tf_op | source)
XLA Modules:
  0.0 159.0 jit_solution(6736220130868759823)
XLA Ops:
  0.6 153.9 %shard_map.187 = (bf16[2,512,1280]{2,1,0:T(8,128)(2,1)S(1)}, bf16[2,512,1280]{2,1,0:T(8,128)(2,1)S(1)}, bf16[2,1280,512]{2,1,0:T(8,128)(2,1)S(1)}, f32[2,64,1280...) custom-call(bf16[1,2,512,1280]{3,2,1,0:T(8,128)(2,1)} %refs_0_.1, ...), custom_call_target="tpu_custom_call" | custom-call | tf_op jit(solution)/shard_map/pallas_call | solution.py:359
  154.6 4.4 %shard_map.188 = (bf16[2,512,1280]{2,1,0:T(8,128)(2,1)}, bf16[2,512,1280]{2,1,0:T(8,128)(2,1)}, bf16[2,1280,512]{2,1,0:T(8,128)(2,1)}, f32[2,64,1280]{2,1,0:T(8,...) custom-call(bf16[2,512,1280]{2,1,0:T(8,128)(2,1)S(1)} %get-tuple-ele, ...), custom_call_target="tpu_custom_call" | custom-call | tf_op jit(solution)/shard_map/pallas_call | solution.py:377

commit v13 on v12

--- a/solution.py
+++ b/solution.py
@@ -10,8 +10,8 @@
 AXIS = "dp"
 MESH = pl.DeviceIdType.MESH
 ROWS, LANES = 16, 128
-LEFT_OUT = {True: 33, False: 16}
-AROUND = {True: 48, False: 80}
+LEFT_OUT = {True: 28, False: 16}
+AROUND = {True: 80, False: 96}
 
 def adamw(w, m, v, g):
     m = 0.9 * m + 0.1 * g
@@ -81,9 +81,10 @@
             device_id_type=MESH,
         )
 
-    def first_copy(i, layer, skip=0):
+    def first_copy(i, layer, skip=0, loaded=False):
         rightward, count = layer < half, plan.block[i] - skip
-        source = terms[i].at[0, layer, pl.ds(pl.multiple_of(behind(rightward, 1) * plan.block[i] + skip, ROWS), count)]
+        part = pl.ds(pl.multiple_of(behind(rightward, 1) * plan.block[i] + skip, ROWS), count)
+        source = held[i].at[layer, part] if loaded else terms[i].at[0, layer, part]
         return send(rightward, source, first[i].at[layer, pl.ds(skip, count)], first_send.at[i, layer], first_recv.at[i, layer])
 
     split = {(plan.order[0], 0): True, (plan.order[0], half): False}
@@ -101,12 +102,12 @@
         pl.when(shorter)(lambda: do(short()))
         pl.when(jnp.logical_not(shorter))(lambda: do(full()))
 
-    def first_of(i, layer, shorter, do):
+    def first_of(i, layer, shorter, do, loaded=False):
         if (i, layer) in split:
             rightward = split[i, layer]
-            either(shorter[rightward], lambda: first_copy(i, layer, AROUND[rightward]), lambda: first_copy(i, layer), do)
+            either(shorter[rightward], lambda: first_copy(i, layer, AROUND[rightward], loaded), lambda: first_copy(i, layer, 0, loaded), do)
         else:
-            do(first_copy(i, layer))
+            do(first_copy(i, layer, 0, loaded))
 
     def sum_copy(at, step):
         rightward, tile, count, _ = plan.copies[at]
@@ -126,7 +127,7 @@
 
     def load(i, layer, steps):
         part = rows(i, behind(layer < half, steps))
-        return pltpu.make_async_copy(terms[i].at[0, layer, part], held[i].at[layer, part], held_sem.at[i, layer, steps - 2])
+        return pltpu.make_async_copy(terms[i].at[0, layer, part], held[i].at[layer, part], held_sem.at[i, layer, steps - 1])
 
     def own_load(i):
         return pltpu.make_async_copy(weights[i].at[:, rows(i, me)], own[i], own_sem.at[i])
@@ -159,10 +160,21 @@
     def _():
         pl.semaphore_signal(barrier, inc=1, device_id={AXIS: left}, device_id_type=MESH)
 
-    def start(rightward):
+    def first_loads(rightward):
         for i, layer in every:
             if (layer < half) == rightward:
-                first_of(i, layer, splits, lambda copy: copy.start())
+                load(i, layer, 1).start()
+
+    def start(rightward, loaded):
+        for i, layer in every:
+            if (layer < half) == rightward:
+                if loaded:
+                    load(i, layer, 1).wait()
+                first_of(i, layer, splits, lambda copy: copy.start(), loaded)
+
+    inner, ends_of_line = me < n - 2, (me == 0) | (me == n - 1)
+    pl.when(inner)(lambda: first_loads(True))
+    pl.when(ends_of_line)(lambda: first_loads(False))
 
     @pl.when(me > 0)
     def _():
@@ -171,23 +183,22 @@
     @pl.when((me > 0) & (me < n - 1))
     def _():
         pl.semaphore_signal(entered.at[1], inc=1, device_id={AXIS: left}, device_id_type=MESH)
-        start(False)
+        start(False, False)
 
     @pl.when(me >= n - 2)
     def _():
         pl.semaphore_signal(entered.at[0], inc=1, device_id={AXIS: right}, device_id_type=MESH)
-        start(True)
-
-    @pl.when(me < n - 2)
+        start(True, False)
+
+    @pl.when(inner)
     def _():
         pl.semaphore_wait(entered.at[1], 1)
-        start(True)
-
-
-    @pl.when((me == 0) | (me == n - 1))
+        start(True, True)
+
+    @pl.when(ends_of_line)
     def _():
         pl.semaphore_wait(entered.at[0], 1)
-        start(False)
+        start(False, True)
 
     for (i, layer), rightward in split.items():
 
@@ -364,7 +375,7 @@
             scratch_shapes=[pltpu.VMEM(w.shape, kind) for w in weights]
             + [pltpu.VMEM(one.shape, kind) for one in m + m]
             + [pltpu.VMEM((n - 1, plan.tiles, ROWS, LANES), kind), pltpu.VMEM((n, plan.tiles, ROWS, LANES), kind)]
-            + [pltpu.SemaphoreType.REGULAR((2,)), dma((3, layers, n - 1)), dma((3,)), dma((3,)), dma((3,))]
+            + [pltpu.SemaphoreType.REGULAR((2,)), dma((3, layers, n)), dma((3,)), dma((3,)), dma((3,))]
             + [dma((3, layers))] * 2
             + [dma((n - 2, len(plan.copies)))] * 2
             + [dma((n - 1, len(plan.copies)))] * 2

time: 159 us -> 160 us (level)
  no operation moved by 1% of the time
where the time goes in v13:
time: 160 us; the launch traced here: 159 us
  Pallas kernels  158 us (99%)
    pallas_call x1, Pallas kernels, step(): pl.pallas_call(functools.partial(kernel, n, plan), out_shape=tuple((pltpu...  154 us
    pallas_call x1, Pallas kernels, step(): pl.pallas_call(put, out_shape=tuple((pltpu.HBM(one.shape, one.dtype) for...  4.42 us

profile of v13, /device:TPU:22, one launch (start us, length us, event | category | flops | bytes accessed | tf_op | source)
XLA Modules:
  0.0 158.6 jit_solution(15480564836172442953)
XLA Ops:
  0.6 153.6 %shard_map.187 = (bf16[2,512,1280]{2,1,0:T(8,128)(2,1)S(1)}, bf16[2,512,1280]{2,1,0:T(8,128)(2,1)S(1)}, bf16[2,1280,512]{2,1,0:T(8,128)(2,1)S(1)}, f32[2,64,1280...) custom-call(bf16[1,2,512,1280]{3,2,1,0:T(8,128)(2,1)} %refs_0_.1, ...), custom_call_target="tpu_custom_call" | custom-call | tf_op jit(solution)/shard_map/pallas_call | solution.py:370
  154.2 4.4 %shard_map.188 = (bf16[2,512,1280]{2,1,0:T(8,128)(2,1)}, bf16[2,512,1280]{2,1,0:T(8,128)(2,1)}, bf16[2,1280,512]{2,1,0:T(8,128)(2,1)}, f32[2,64,1280]{2,1,0:T(8,...) custom-call(bf16[2,512,1280]{2,1,0:T(8,128)(2,1)S(1)} %get-tuple-ele, ...), custom_call_target="tpu_custom_call" | custom-call | tf_op jit(solution)/shard_map/pallas_call | solution.py:388

commit v14 on v12

--- a/solution.py
+++ b/solution.py
@@ -10,8 +10,8 @@
 AXIS = "dp"
 MESH = pl.DeviceIdType.MESH
 ROWS, LANES = 16, 128
-LEFT_OUT = {True: 33, False: 16}
-AROUND = {True: 48, False: 80}
+LEFT_OUT = {True: 28, False: 16}
+AROUND = {True: 80, False: 80}
 
 def adamw(w, m, v, g):
     m = 0.9 * m + 0.1 * g
@@ -311,13 +311,13 @@
         either(shorter, lambda: out_copy(at, n - 2, left_out), lambda: out_copy(at, n - 2), do)
 
     def sends_shorter(at):
-        return me == (n - 1 if plan.copies[at][0] else 0)
+        return me == n - 1 if plan.copies[at][0] else (me == 0) | (me == n - 1)
 
     def gets_shorter(at):
-        return me == (0 if plan.copies[at][0] else n - 1)
+        return me == 0 if plan.copies[at][0] else (me == n - 1) | (me == n - 2)
 
     def sends_end(at):
-        return me == (1 if plan.copies[at][0] else n - 2)
+        return me == 1 if plan.copies[at][0] else (me == n - 2) | (me == n - 3)
 
     for at in range(len(plan.copies)):
         out_copy(at, n - 3).wait_recv()
@@ -342,8 +342,8 @@
 def put(*refs):
     count = len(refs) // 2
     copies = [pltpu.make_async_copy(refs[i], refs[count + i], refs[-1].at[i]) for i in range(count)]
-    for copy in copies:
-        copy.start()
+    for i, copy in enumerate(copies):
+        copy.start(priority=i % 2)
     for copy in copies:
         copy.wait()
 

time: 159 us -> 159 us (level)
  no operation moved by 1% of the time
where the time goes in v14:
time: 159 us
  Pallas kernels  158 us (99%)
    pallas_call x1, Pallas kernels, step(): pl.pallas_call(functools.partial(kernel, n, plan), out_shape=tuple((pltpu...  153 us
    pallas_call x1, Pallas kernels, step(): pl.pallas_call(put, out_shape=tuple((pltpu.HBM(one.shape, one.dtype) for...  4.42 us

profile of v14, /device:TPU:22, one launch (start us, length us, event | category | flops | bytes accessed | tf_op | source)
XLA Modules:
  0.0 158.6 jit_solution(7015290673966621363)
XLA Ops:
  0.6 153.5 %shard_map.187 = (bf16[2,512,1280]{2,1,0:T(8,128)(2,1)S(1)}, bf16[2,512,1280]{2,1,0:T(8,128)(2,1)S(1)}, bf16[2,1280,512]{2,1,0:T(8,128)(2,1)S(1)}, f32[2,64,1280...) custom-call(bf16[1,2,512,1280]{3,2,1,0:T(8,128)(2,1)} %refs_0_.1, ...), custom_call_target="tpu_custom_call" | custom-call | tf_op jit(solution)/shard_map/pallas_call | solution.py:359
  154.1 4.4 %shard_map.188 = (bf16[2,512,1280]{2,1,0:T(8,128)(2,1)}, bf16[2,512,1280]{2,1,0:T(8,128)(2,1)}, bf16[2,1280,512]{2,1,0:T(8,128)(2,1)}, f32[2,64,1280]{2,1,0:T(8,...) custom-call(bf16[2,512,1280]{2,1,0:T(8,128)(2,1)S(1)} %get-tuple-ele, ...), custom_call_target="tpu_custom_call" | custom-call | tf_op jit(solution)/shard_map/pallas_call | solution.py:377

commit v15 on v14

--- a/solution.py
+++ b/solution.py
@@ -10,7 +10,7 @@
 AXIS = "dp"
 MESH = pl.DeviceIdType.MESH
 ROWS, LANES = 16, 128
-LEFT_OUT = {True: 28, False: 16}
+LEFT_OUT = {True: 28, False: 11}
 AROUND = {True: 80, False: 80}
 
 def adamw(w, m, v, g):
@@ -342,8 +342,8 @@
 def put(*refs):
     count = len(refs) // 2
     copies = [pltpu.make_async_copy(refs[i], refs[count + i], refs[-1].at[i]) for i in range(count)]
-    for i, copy in enumerate(copies):
-        copy.start(priority=i % 2)
+    for copy in copies:
+        copy.start()
     for copy in copies:
         copy.wait()
 

time: 159 us -> 159 us (level)
  no operation moved by 1% of the time
where the time goes in v15:
time: 159 us
  Pallas kernels  158 us (99%)
    pallas_call x1, Pallas kernels, step(): pl.pallas_call(functools.partial(kernel, n, plan), out_shape=tuple((pltpu...  154 us
    pallas_call x1, Pallas kernels, step(): pl.pallas_call(put, out_shape=tuple((pltpu.HBM(one.shape, one.dtype) for...  4.42 us

profile of v15, /device:TPU:22, one launch (start us, length us, event | category | flops | bytes accessed | tf_op | source)
XLA Modules:
  0.0 158.8 jit_solution(10315687867119719695)
XLA Ops:
  0.6 153.7 %shard_map.187 = (bf16[2,512,1280]{2,1,0:T(8,128)(2,1)S(1)}, bf16[2,512,1280]{2,1,0:T(8,128)(2,1)S(1)}, bf16[2,1280,512]{2,1,0:T(8,128)(2,1)S(1)}, f32[2,64,1280...) custom-call(bf16[1,2,512,1280]{3,2,1,0:T(8,128)(2,1)} %refs_0_.1, ...), custom_call_target="tpu_custom_call" | custom-call | tf_op jit(solution)/shard_map/pallas_call | solution.py:359
  154.4 4.4 %shard_map.188 = (bf16[2,512,1280]{2,1,0:T(8,128)(2,1)}, bf16[2,512,1280]{2,1,0:T(8,128)(2,1)}, bf16[2,1280,512]{2,1,0:T(8,128)(2,1)}, f32[2,64,1280]{2,1,0:T(8,...) custom-call(bf16[2,512,1280]{2,1,0:T(8,128)(2,1)S(1)} %get-tuple-ele, ...), custom_call_target="tpu_custom_call" | custom-call | tf_op jit(solution)/shard_map/pallas_call | solution.py:377
